TPU v7x, 32 devices: a whole 2x2x4 slice. The times are simulated.
32 devices in a mesh: frames: 2 (over core), pix: 16 (over z, y, x).
Axes of the slice: x: 2, y: 2, z: 4, core: 2. Of those that a mesh axis runs over, the one named last changes fastest.
Arguments:
- frames: float32 [256, 32768], P('frames', 'pix'), may hold values from -6 to 6
Outputs:
- sketch: float32 [128, 32768], P(None, 'pix')
- projected: float32 [256, 32768], P('frames', 'pix')
All inputs are finite; a program needn't handle non-finite values.
Results may differ from a plain program's by a relative error of at most 0.0003.
Values sent between devices are 32-bit elements; how exact they have to be, the bound alone decides.
No kernel may reach another device: no remote copies, remote signals or barrier semaphores. Data moves between devices by JAX's collectives and lax.ppermute only.
A program may use at most 64 MiB of HBM per device.

v0:
```python
import jax
import jax.numpy as jnp
from jax import lax
from jax.experimental import pallas as pl
from jax.experimental.pallas import tpu as pltpu
from jax.sharding import PartitionSpec as P

PANEL = 32


def nn(left, right):
    return lax.dot_general(left, right, (((1,), (0,)), ((), ())), precision=lax.Precision.HIGHEST, preferred_element_type=jnp.float32)


def nt(left, right):
    return lax.dot_general(left, right, (((1,), (1,)), ((), ())), precision=lax.Precision.HIGHEST, preferred_element_type=jnp.float32)


def parity(index):
    for shift in (16, 8, 4, 2, 1):
        index = index ^ (index >> shift)
    return index & 1


def half_of(core_axis, axis):
    return lax.axis_index(core_axis) ^ parity(lax.axis_index(axis))


def sum_over(block, axis, core_axis):
    count = lax.axis_size(axis)
    steps = [1 << k for k in range(count.bit_length() - 1)]
    steps = steps[-1:] + steps[:-1]
    for k in range(len(steps)):
        swapped = k ^ 1 if k ^ 1 < len(steps) else k
        route = []
        for core in range(2):
            for i in range(count):
                step = steps[swapped if core ^ parity(i) else k]
                route.append((core * count + i, (1 - core) * count + (i ^ step)))
        block = block + lax.ppermute(block, (core_axis, axis), route)
    return block


def across(block, column):
    return jnp.broadcast_to(block[:, column : column + 1], block.shape)


def down(block, row):
    return jnp.broadcast_to(block[row : row + 1, :], block.shape)


def eliminate(diag, start, rows):
    many = len(diag)
    size = 8 * many
    sub = lax.broadcasted_iota(jnp.int32, diag[0].shape, 0)
    cols = {(c, r): across(diag[r], start + c) for c in range(size) for r in range(c // 8, many)}
    rows = list(rows)
    for j in range(size):
        strip, at = divmod(j, 8)
        inverse = lax.rsqrt(down(cols[j, strip], at))
        low = {r: cols[j, r] * inverse for r in range(strip, many)}
        for c in range(j + 1, size):
            factor = down(low[c // 8], c % 8)
            for r in range(c // 8, many):
                cols[c, r] = cols[c, r] - low[r] * factor
        row = down(rows[strip], at) * inverse
        under = jnp.where(sub > at, low[strip], 0.0)
        rows[strip] = jnp.where(sub == at, row, rows[strip] - under * row)
        for r in range(strip + 1, many):
            rows[r] = rows[r] - low[r] * row
    return rows


def inverse_factors(grams):
    size = grams[0].shape[0]
    column = lax.broadcasted_iota(jnp.int32, (8, size), 1)
    sub = lax.broadcasted_iota(jnp.int32, (8, size), 0)
    done = [[] for _ in grams]
    for start in range(0, size, PANEL):
        for k, gram in enumerate(grams):
            offsets = range(start, start + PANEL, 8)
            mine = [gram[i : i + 8] for i in offsets]
            unit = [(column == sub + i).astype(jnp.float32) for i in offsets]
            if start:
                above = jnp.concatenate(done[k] + [jnp.zeros((size - start, size), jnp.float32)], axis=0)
                low = nt(jnp.concatenate(mine, axis=0), above)
                padded = [jnp.zeros((start, size), jnp.float32), low]
                if size - start - PANEL:
                    padded.append(jnp.zeros((size - start - PANEL, size), jnp.float32))
                square = nt(low, jnp.concatenate(padded, axis=0))
                back = nn(low, above)
                mine = [v - square[8 * i : 8 * i + 8] for i, v in enumerate(mine)]
                unit = [v - back[8 * i : 8 * i + 8] for i, v in enumerate(unit)]
            done[k] += eliminate(mine, start, unit)
    return [jnp.concatenate(d, axis=0) for d in done]


def total(block):
    return jnp.sum(jnp.sum(block, axis=0, keepdims=True), axis=1, keepdims=True)


def transform(lower_gram, cross, upper_gram, is_upper):
    kept = lower_gram.shape[0]
    normal = nt(lower_gram, lower_gram) + nt(cross, cross)
    beside = nn(lower_gram, cross) + nn(cross, upper_gram)
    (inverse,) = inverse_factors([normal])
    basis = nn(inverse, lower_gram), nn(inverse, cross)
    image = nn(inverse, normal), nn(inverse, beside)
    reduced = nt(image[0], basis[0]) + nt(image[1], basis[1])
    delta = total(image[0] * basis[0] + image[1] * basis[1]) / kept
    on_diagonal = lax.broadcasted_iota(jnp.int32, reduced.shape, 0) == lax.broadcasted_iota(jnp.int32, reduced.shape, 1)
    root, damped = inverse_factors([reduced, reduced + jnp.where(on_diagonal, delta, 0.0)])
    shrunk = nt(reduced, damped)
    whitened = nn(root, basis[0]), nn(root, basis[1])
    mixing = nn(shrunk, whitened[0]), nn(shrunk, whitened[1])
    left = jnp.where(is_upper, cross.T, lower_gram)
    right = jnp.where(is_upper, upper_gram, cross)
    scaling = 4.0 * kept / (total(shrunk * shrunk) + 1e-06)
    coeffs = nt(nt(left, whitened[0]) + nt(right, whitened[1]), shrunk) * scaling
    return mixing, coeffs


def split(block):
    high = block.astype(jnp.bfloat16)
    return high, (block - high.astype(jnp.float32)).astype(jnp.bfloat16)


def stacked(block):
    high, low = split(block)
    return jnp.concatenate([high, low], axis=0), high


def product(left, right_high, right_low):
    both, high = left
    rows = high.shape[0]
    out = jnp.dot(both, right_high, preferred_element_type=jnp.float32)
    return out[:rows] + (out[rows:] + jnp.dot(high, right_low, preferred_element_type=jnp.float32))


def positions(size):
    return (lax.broadcasted_iota(jnp.int32, (size, size), axis) for axis in (0, 1))


def own_gram_kernel(own_ref, gram_ref, kept_ref):
    own = own_ref[...]
    kept_ref[...] = own
    gram_ref[...] = nt(own, own)


def pack_kernel(own_ref, other_ref, own_gram_ref, packed_ref):
    kept = own_ref.shape[0]
    is_upper = lax.axis_index("frames") == 1
    is_cross = half_of("frames", "pix") == 0
    own, other = own_ref[...], other_ref[...]
    left = jnp.where(is_cross & ~is_upper, own, other)
    right = jnp.where(is_cross & is_upper, own, other)
    fresh = nt(left, right)
    row, column = positions(kept)
    own_gram = own_gram_ref[...]
    upper_gram = jnp.where(is_upper, own_gram, fresh)
    mixed = jnp.where(row >= column, jnp.where(is_upper, fresh, own_gram), upper_gram)
    packed_ref[:kept] = jnp.where(is_cross, fresh, mixed)
    diagonal = jnp.sum(jnp.where(row == column, upper_gram, 0.0), axis=0, keepdims=True)
    packed_ref[kept:] = jnp.broadcast_to(diagonal, (8, kept))


def unpack(packed):
    kept = packed.shape[1]
    row, column = positions(kept)
    mixed = packed[:kept]
    turned = mixed.T
    lower_gram = jnp.where(row >= column, mixed, turned)
    upper_gram = jnp.where(row < column, mixed, jnp.where(row > column, turned, packed[kept : kept + 1]))
    return lower_gram, upper_gram


def packed_grams(own, other):
    kept, width = own.shape
    whole = pl.BlockSpec(memory_space=pltpu.VMEM)
    grant = pltpu.CompilerParams(vmem_limit_bytes=16 << 20)
    own_gram, own = pl.pallas_call(
        own_gram_kernel,
        in_specs=[whole],
        out_specs=(whole, whole),
        out_shape=(jax.ShapeDtypeStruct((kept, kept), jnp.float32), jax.ShapeDtypeStruct((kept, width), jnp.float32)),
        compiler_params=grant,
        cost_estimate=pl.CostEstimate(flops=12 * kept * kept * width, bytes_accessed=4 * kept * width, transcendentals=0),
    )(own)
    packed = pl.pallas_call(
        pack_kernel,
        in_specs=[whole] * 3,
        out_specs=whole,
        out_shape=jax.ShapeDtypeStruct((kept + 8, kept), jnp.float32),
        compiler_params=grant,
        cost_estimate=pl.CostEstimate(flops=12 * kept * kept * width, bytes_accessed=8 * kept * width, transcendentals=0),
    )(own, other, own_gram)
    return packed, own


def finish_kernel(summed_ref, given_ref, high_ref, low_ref, sketch_ref, projected_ref, sketch_buf, projected_buf, sems):
    kept, width = sketch_buf.shape
    is_upper = lax.axis_index("frames") == 1
    has_cross = half_of("frames", "pix") == 0
    cross = jnp.where(has_cross, summed_ref[:kept], given_ref[:kept])
    lower_gram, upper_gram = unpack(jnp.where(has_cross, given_ref[...], summed_ref[...]))
    (first, second), coeffs = transform(lower_gram, cross, upper_gram, is_upper)
    mixing = stacked(jnp.concatenate([jnp.where(is_upper, second, first), jnp.where(is_upper, first, second)], axis=1))
    coeffs = stacked(coeffs)
    block = min(width, 512)
    copies = []
    for k in range(width // block):
        columns = pl.ds(k * block, block)
        sketch = product(mixing, high_ref[:, columns], low_ref[:, columns])
        sketch_buf[:, columns] = sketch
        copies.append(pltpu.make_async_copy(sketch_buf.at[:, columns], sketch_ref.at[:, columns], sems.at[2 * k]))
        copies[-1].start()
        projected_buf[:, columns] = product(coeffs, *split(sketch))
        copies.append(pltpu.make_async_copy(projected_buf.at[:, columns], projected_ref.at[:, columns], sems.at[2 * k + 1]))
        copies[-1].start()
    for copy in copies:
        copy.wait()


def finish(summed, given, high, low):
    width = high.shape[1]
    kept = high.shape[0] // 2
    whole = pl.BlockSpec(memory_space=pltpu.VMEM)
    return pl.pallas_call(
        finish_kernel,
        in_specs=[whole] * 4,
        out_specs=(pl.BlockSpec(memory_space=pl.ANY),) * 2,
        out_shape=(jax.ShapeDtypeStruct((kept, width), jnp.float32),) * 2,
        scratch_shapes=[pltpu.VMEM((kept, width), jnp.float32)] * 2 + [pltpu.SemaphoreType.DMA((2 * max(1, width // 512),))],
        compiler_params=pltpu.CompilerParams(vmem_limit_bytes=24 << 20),
    )(summed, given, high, low)


def local(frames):
    other = lax.ppermute(frames, "frames", [(0, 1), (1, 0)])
    packed, own = packed_grams(frames, other)
    summed = sum_over(packed, "pix", "frames")
    given = lax.ppermute(summed, "frames", [(0, 1), (1, 0)])
    rows = jnp.concatenate([own, other], axis=0)
    high = lax.reduce_precision(rows, 8, 7)
    low = (rows - high).astype(jnp.bfloat16)
    return finish(summed, given, high.astype(jnp.bfloat16), low)


def solution(mesh):
    count = mesh.shape["pix"]
    if mesh.shape["frames"] != 2 or count & (count - 1):
        raise ValueError("mesh shape")
    return jax.shard_map(
        local,
        mesh=mesh,
        in_specs=(P("frames", "pix"),),
        out_specs=(P(None, "pix"), P("frames", "pix")),
        check_vma=False,
    )
```

profile of v0, /device:TPU:0, one launch (start us, length us, event | category | flops | bytes accessed | tf_op | source)
XLA Modules:
  0.0 37.2 jit_solution(5483489830868893019)
XLA Ops:
  0.6 0.6 %collective-permute-start = (f32[128,2048]{1,0:T(8,128)}, f32[128,2048]{1,0:T(8,128)S(1)}, u32[]{:S(2)}, u32[]{:S(2)}) collective-permute-start(f32[128,2048]{1,0:T(8,128)} %own_ref.1), channel_id=1, source_target_pairs={{0,16},{16,0},{1,17},{17,1},{2,18},{18,2},{3,19},{19,3},{4,20},{20... | collective-permute-start | bytes 3145736 | tf_op jit(solution)/shard_map/ppermute | solution.py:239
  1.2 0.0 copy-start
  1.2 1.2 %copy-done = f32[128,2048]{1,0:T(8,128)S(1)} copy-done((f32[128,2048]{1,0:T(8,128)S(1)}, f32[128,2048]{1,0:T(8,128)}, u32[]{:S(2)}) %copy-start) | copy-done | bytes 1048600
  2.4 1.1 %shard_map.30 = (f32[128,128]{1,0:T(8,128)S(1)}, f32[128,2048]{1,0:T(8,128)S(1)}) custom-call(f32[128,2048]{1,0:T(8,128)S(1)} %copy-done), custom_call_target="tpu_custom_call" | custom-call | flops 402653184 | bytes 1048576 | tf_op jit(solution)/shard_map/pallas_call | solution.py:181
  3.5 0.2 collective-permute-done.other_ref
  3.7 1.1 %shard_map.31 = f32[136,128]{1,0:T(8,128)S(1)} custom-call(f32[128,2048]{1,0:T(8,128)S(1)} %get-tuple-element.4.own_ref, f32[128,2048]{1,0:T(8,128)S(1)} %collective-permute-done.other_ref, f32[128,128]{1,0:T(8,128)S(1)} %get-tuple-element.5.own_gram_ref), custom_call_target="tpu_custom_call" | custom-call | flops 402653184 | bytes 2097152 | tf_op jit(solution)/shard_map/pallas_call | solution.py:189
  4.8 3.8 %collective-permute-start.1 = (f32[136,128]{1,0:T(8,128)S(1)}, f32[136,128]{1,0:T(8,128)S(1)}, u32[]{:S(2)}, u32[]{:S(2)}) collective-permute-start(f32[136,128]{1,0:T(8,128)S(1)} %shard_map.31), channel_id=1, source_target_pairs={{0,24},{1,16},{2,19},{3,27},{4,21},{5,29},{6,30},{7,22},{8,25},{9,... | collective-permute-start | bytes 208904 | tf_op jit(solution)/shard_map/ppermute | solution.py:40
  8.6 2.0 %collective-permute-done.1 = f32[136,128]{1,0:T(8,128)S(1)} collective-permute-done((f32[136,128]{1,0:T(8,128)S(1)}, f32[136,128]{1,0:T(8,128)S(1)}, u32[]{:S(2)}, u32[]{:S(2)}) %collective-permute-start.1) | collective-permute-done | bytes 69664 | tf_op jit(solution)/shard_map/ppermute | solution.py:40
  10.6 1.6 %collective-permute-start.2 = (f32[136,128]{1,0:T(8,128)S(1)}, f32[136,128]{1,0:T(8,128)S(1)}, u32[]{:S(2)}, u32[]{:S(2)}) collective-permute-start(f32[136,128]{1,0:T(8,128)S(1)} %add.12), channel_id=1, source_target_pairs={{0,17},{1,25},{2,26},{3,18},{4,28},{5,20},{6,23},{7,31},{8,16},{9,... | collective-permute-start | bytes 208904 | tf_op jit(solution)/shard_map/ppermute | solution.py:40
  12.2 2.2 %collective-permute-done.2 = f32[136,128]{1,0:T(8,128)S(1)} collective-permute-done((f32[136,128]{1,0:T(8,128)S(1)}, f32[136,128]{1,0:T(8,128)S(1)}, u32[]{:S(2)}, u32[]{:S(2)}) %collective-permute-start.2) | collective-permute-done | bytes 69664 | tf_op jit(solution)/shard_map/ppermute | solution.py:40
  14.4 1.6 %collective-permute-start.3 = (f32[136,128]{1,0:T(8,128)S(1)}, f32[136,128]{1,0:T(8,128)S(1)}, u32[]{:S(2)}, u32[]{:S(2)}) collective-permute-start(f32[136,128]{1,0:T(8,128)S(1)} %add.13), channel_id=1, source_target_pairs={{0,18},{1,21},{2,22},{3,17},{4,16},{5,23},{6,20},{7,19},{8,28},{9,... | collective-permute-start | bytes 208904 | tf_op jit(solution)/shard_map/ppermute | solution.py:40
  16.0 0.1 constant_dynamic-update-slice_fusion.1
  16.1 2.1 %collective-permute-done.3 = f32[136,128]{1,0:T(8,128)S(1)} collective-permute-done((f32[136,128]{1,0:T(8,128)S(1)}, f32[136,128]{1,0:T(8,128)S(1)}, u32[]{:S(2)}, u32[]{:S(2)}) %collective-permute-start.3) | collective-permute-done | bytes 69664 | tf_op jit(solution)/shard_map/ppermute | solution.py:40
  18.2 1.7 %collective-permute-start.4 = (f32[136,128]{1,0:T(8,128)S(1)}, f32[136,128]{1,0:T(8,128)S(1)}, u32[]{:S(2)}, u32[]{:S(2)}) collective-permute-start(f32[136,128]{1,0:T(8,128)S(1)} %add.14), channel_id=1, source_target_pairs={{0,20},{1,19},{2,16},{3,23},{4,22},{5,17},{6,18},{7,21},{8,26},{9,... | collective-permute-start | bytes 208904 | tf_op jit(solution)/shard_map/ppermute | solution.py:40
  19.9 0.1 constant_dynamic-update-slice_fusion
  20.0 2.0 %collective-permute-done.4 = f32[136,128]{1,0:T(8,128)S(1)} collective-permute-done((f32[136,128]{1,0:T(8,128)S(1)}, f32[136,128]{1,0:T(8,128)S(1)}, u32[]{:S(2)}, u32[]{:S(2)}) %collective-permute-start.4) | collective-permute-done | bytes 69664 | tf_op jit(solution)/shard_map/ppermute | solution.py:40
  22.0 0.5 %collective-permute-start.5 = (f32[136,128]{1,0:T(8,128)S(1)}, f32[136,128]{1,0:T(8,128)S(1)}, u32[]{:S(2)}, u32[]{:S(2)}) collective-permute-start(f32[136,128]{1,0:T(8,128)S(1)} %add.15.summed_ref), channel_id=1, source_target_pairs={{0,16},{16,0},{1,17},{17,1},{2,18},{18,2},{3,19},{19,3},{4,20},{20... | collective-permute-start | bytes 208904 | tf_op jit(solution)/shard_map/ppermute | solution.py:242
  22.5 0.4 %fusion = (bf16[256,2048]{1,0:T(8,128)(2,1)S(1)}, bf16[256,2048]{1,0:T(8,128)(2,1)S(1)}) fusion(f32[256,2048]{1,0:T(8,128)S(1)} %constant_dynamic-update-slice_fusion), kind=kLoop, calls=%fused_computation.2 | loop fusion | flops 2097152 | bytes 4194304 | tf_op jit(solution)/shard_map/convert_element_type | solution.py:245
  22.9 0.5 %collective-permute-done.5.given_ref = f32[136,128]{1,0:T(8,128)S(1)} collective-permute-done((f32[136,128]{1,0:T(8,128)S(1)}, f32[136,128]{1,0:T(8,128)S(1)}, u32[]{:S(2)}, u32[]{:S(2)}) %collective-permute-start.5) | collective-permute-done | bytes 69664 | tf_op jit(solution)/shard_map/ppermute | solution.py:242
  23.5 13.7 %shard_map.32 = (f32[128,2048]{1,0:T(8,128)}, f32[128,2048]{1,0:T(8,128)}) custom-call(f32[136,128]{1,0:T(8,128)S(1)} %add.15.summed_ref, f32[136,128]{1,0:T(8,128)S(1)} %collective-permute-done.5.given_ref, bf16[256,2048]{1,0:T(8,128)(2,1)S(1)} %get-tuple-element.7.high_ref, bf16[256,2048]{1,0:T(8,128)(2,1)S(1)} %get-tuple-element.6.low_ref), custom_call_target="tpu_custom_call" | custom-call | tf_op jit(solution)/shard_map/pallas_call | solution.py:228
  (4 shorter events, 0.0 us)
Async XLA Ops:
  0.6 3.1 %collective-permute-start = (f32[128,2048]{1,0:T(8,128)}, f32[128,2048]{1,0:T(8,128)S(1)}, u32[]{:S(2)}, u32[]{:S(2)}) collective-permute-start(f32[128,2048]{1,0:T(8,128)} %own_ref.1), channel_id=1, source_target_pairs={{0,16},{16,0},{1,17},{17,1},{2,18},{18,2},{3,19},{19,3},{4,20},{20... | collective-permute-start | bytes 3145736 | tf_op jit(solution)/shard_map/ppermute | solution.py:239
  1.2 1.2 %copy-start = (f32[128,2048]{1,0:T(8,128)S(1)}, f32[128,2048]{1,0:T(8,128)}, u32[]{:S(2)}) copy-start(f32[128,2048]{1,0:T(8,128)} %own_ref.1) | copy-start | bytes 3145732
  4.8 5.7 %collective-permute-start.1 = (f32[136,128]{1,0:T(8,128)S(1)}, f32[136,128]{1,0:T(8,128)S(1)}, u32[]{:S(2)}, u32[]{:S(2)}) collective-permute-start(f32[136,128]{1,0:T(8,128)S(1)} %shard_map.31), channel_id=1, source_target_pairs={{0,24},{1,16},{2,19},{3,27},{4,21},{5,29},{6,30},{7,22},{8,25},{9,... | collective-permute-start | bytes 208904 | tf_op jit(solution)/shard_map/ppermute | solution.py:40
  10.6 3.8 %collective-permute-start.2 = (f32[136,128]{1,0:T(8,128)S(1)}, f32[136,128]{1,0:T(8,128)S(1)}, u32[]{:S(2)}, u32[]{:S(2)}) collective-permute-start(f32[136,128]{1,0:T(8,128)S(1)} %add.12), channel_id=1, source_target_pairs={{0,17},{1,25},{2,26},{3,18},{4,28},{5,20},{6,23},{7,31},{8,16},{9,... | collective-permute-start | bytes 208904 | tf_op jit(solution)/shard_map/ppermute | solution.py:40
  14.4 3.8 %collective-permute-start.3 = (f32[136,128]{1,0:T(8,128)S(1)}, f32[136,128]{1,0:T(8,128)S(1)}, u32[]{:S(2)}, u32[]{:S(2)}) collective-permute-start(f32[136,128]{1,0:T(8,128)S(1)} %add.13), channel_id=1, source_target_pairs={{0,18},{1,21},{2,22},{3,17},{4,16},{5,23},{6,20},{7,19},{8,28},{9,... | collective-permute-start | bytes 208904 | tf_op jit(solution)/shard_map/ppermute | solution.py:40
  18.2 3.8 %collective-permute-start.4 = (f32[136,128]{1,0:T(8,128)S(1)}, f32[136,128]{1,0:T(8,128)S(1)}, u32[]{:S(2)}, u32[]{:S(2)}) collective-permute-start(f32[136,128]{1,0:T(8,128)S(1)} %add.14), channel_id=1, source_target_pairs={{0,20},{1,19},{2,16},{3,23},{4,22},{5,17},{6,18},{7,21},{8,26},{9,... | collective-permute-start | bytes 208904 | tf_op jit(solution)/shard_map/ppermute | solution.py:40
  22.0 1.5 %collective-permute-start.5 = (f32[136,128]{1,0:T(8,128)S(1)}, f32[136,128]{1,0:T(8,128)S(1)}, u32[]{:S(2)}, u32[]{:S(2)}) collective-permute-start(f32[136,128]{1,0:T(8,128)S(1)} %add.15.summed_ref), channel_id=1, source_target_pairs={{0,16},{16,0},{1,17},{17,1},{2,18},{18,2},{3,19},{19,3},{4,20},{20... | collective-permute-start | bytes 208904 | tf_op jit(solution)/shard_map/ppermute | solution.py:242
where the time goes:
time: 37.4 us; the launch traced here: 37.2 us
  Pallas kernels  15.9 us (43%)
  starting transfers between devices  9.87 us (26%)
  waiting for transfers between devices  8.96 us (24%)
  local copies, waits for them, and re-layouts  1.36 us (4%)
  between operations  0.68 us (2%)
  other arithmetic  0.43 us (1%)
    pallas_call x1, Pallas kernels, finish(): pl.pallas_call(finish_kernel, in_specs=[whole] * 4, out_specs=(pl.BlockSp...  13.7 us
    ppermute x4, starting transfers between devices, sum_over(): block = block + lax.ppermute(block, (core_axis, axis), route)  8.76 us
    ppermute x4, waiting for transfers between devices, sum_over(): block = block + lax.ppermute(block, (core_axis, axis), route)  8.23 us
    unnamed x3, local copies, waits for them, and re-layouts  1.29 us
    pallas_call x1, Pallas kernels, packed_grams(): pl.pallas_call(pack_kernel, in_specs=[whole] * 3, out_specs=whole, out_sh...  1.11 us
    pallas_call x1, Pallas kernels, packed_grams(): pl.pallas_call(own_gram_kernel, in_specs=[whole], out_specs=(whole, whole...  1.05 us
  transfers between devices with their start and end apart: 6, of which 6 were waited for; matrix products, arithmetic and copies ran while one was open for 1% of the time, Pallas kernels for 3%

commit v1 on v0

--- a/solution.py
+++ b/solution.py
@@ -49,50 +49,59 @@
     return jnp.broadcast_to(block[row : row + 1, :], block.shape)
 
 
-def eliminate(diag, start, rows):
+def eliminate(diag, start, carried, group, ahead):
     many = len(diag)
     size = 8 * many
     sub = lax.broadcasted_iota(jnp.int32, diag[0].shape, 0)
-    cols = {(c, r): across(diag[r], start + c) for c in range(size) for r in range(c // 8, many)}
-    rows = list(rows)
+    strips = list(diag)
+    carried = [list(rows) for rows in carried]
+    cols = {}
+    ready = 0
     for j in range(size):
+        if j + ahead >= ready and ready < size:
+            for c in range(ready, ready + group):
+                for r in range(c // 8, many):
+                    cols[c, r] = across(strips[r], start + c)
+            ready += group
         strip, at = divmod(j, 8)
         inverse = lax.rsqrt(down(cols[j, strip], at))
         low = {r: cols[j, r] * inverse for r in range(strip, many)}
-        for c in range(j + 1, size):
+        for c in range(j + 1, ready):
             factor = down(low[c // 8], c % 8)
             for r in range(c // 8, many):
                 cols[c, r] = cols[c, r] - low[r] * factor
-        row = down(rows[strip], at) * inverse
         under = jnp.where(sub > at, low[strip], 0.0)
-        rows[strip] = jnp.where(sub == at, row, rows[strip] - under * row)
-        for r in range(strip + 1, many):
-            rows[r] = rows[r] - low[r] * row
-    return rows
-
-
-def inverse_factors(grams):
+        for rows in carried + ([strips] if ready < size else []):
+            row = down(rows[strip], at) * inverse
+            rows[strip] = jnp.where(sub == at, row, rows[strip] - under * row)
+            for r in range(strip + 1, many):
+                rows[r] = rows[r] - low[r] * row
+    return carried
+
+
+def inverse_factors(grams, group, ahead):
     size = grams[0].shape[0]
+    count, step = size // 8, PANEL // 8
     column = lax.broadcasted_iota(jnp.int32, (8, size), 1)
     sub = lax.broadcasted_iota(jnp.int32, (8, size), 0)
-    done = [[] for _ in grams]
-    for start in range(0, size, PANEL):
-        for k, gram in enumerate(grams):
-            offsets = range(start, start + PANEL, 8)
-            mine = [gram[i : i + 8] for i in offsets]
-            unit = [(column == sub + i).astype(jnp.float32) for i in offsets]
-            if start:
-                above = jnp.concatenate(done[k] + [jnp.zeros((size - start, size), jnp.float32)], axis=0)
-                low = nt(jnp.concatenate(mine, axis=0), above)
-                padded = [jnp.zeros((start, size), jnp.float32), low]
-                if size - start - PANEL:
-                    padded.append(jnp.zeros((size - start - PANEL, size), jnp.float32))
-                square = nt(low, jnp.concatenate(padded, axis=0))
-                back = nn(low, above)
-                mine = [v - square[8 * i : 8 * i + 8] for i, v in enumerate(mine)]
-                unit = [v - back[8 * i : 8 * i + 8] for i, v in enumerate(unit)]
-            done[k] += eliminate(mine, start, unit)
-    return [jnp.concatenate(d, axis=0) for d in done]
+    left = [[gram[8 * i : 8 * i + 8] for i in range(count)] for gram in grams]
+    right = [[(column == sub + 8 * i).astype(jnp.float32) for i in range(count)] for _ in grams]
+    for first in range(0, count, step):
+        rest = first + step
+        for a, z in zip(left, right):
+            block = a[first:rest]
+            if rest == count:
+                (z[first:rest],) = eliminate(block, 8 * first, [z[first:rest]], group, ahead)
+                continue
+            z[first:rest], above = eliminate(block, 8 * first, [z[first:rest], block], group, ahead)
+            above = jnp.concatenate(above, axis=0)
+            both = jnp.concatenate([above, jnp.concatenate(z[first:rest], axis=0)], axis=1)
+            update = nn(above.T[8 * rest :], both)
+            for i in range(rest, count):
+                rows = slice(8 * (i - rest), 8 * (i - rest) + 8)
+                a[i] = a[i] - update[rows, :size]
+                z[i] = z[i] - update[rows, size:]
+    return [jnp.concatenate(z, axis=0) for z in right]
 
 
 def total(block):
@@ -103,13 +112,13 @@
     kept = lower_gram.shape[0]
     normal = nt(lower_gram, lower_gram) + nt(cross, cross)
     beside = nn(lower_gram, cross) + nn(cross, upper_gram)
-    (inverse,) = inverse_factors([normal])
+    (inverse,) = inverse_factors([normal], 16, 6)
     basis = nn(inverse, lower_gram), nn(inverse, cross)
     image = nn(inverse, normal), nn(inverse, beside)
     reduced = nt(image[0], basis[0]) + nt(image[1], basis[1])
     delta = total(image[0] * basis[0] + image[1] * basis[1]) / kept
     on_diagonal = lax.broadcasted_iota(jnp.int32, reduced.shape, 0) == lax.broadcasted_iota(jnp.int32, reduced.shape, 1)
-    root, damped = inverse_factors([reduced, reduced + jnp.where(on_diagonal, delta, 0.0)])
+    root, damped = inverse_factors([reduced, reduced + jnp.where(on_diagonal, delta, 0.0)], 8, 4)
     shrunk = nt(reduced, damped)
     whitened = nn(root, basis[0]), nn(root, basis[1])
     mixing = nn(shrunk, whitened[0]), nn(shrunk, whitened[1])

time: 37.4 us -> 35.3 us (0.944)
  Pallas kernels: 15.9 us -> 13.8 us
    pallas_call x1, Pallas kernels: 13.7 us -> 11.7 us  [finish(): pl.pallas_call(finish_kernel, in_specs=[whole] * 4, out_specs=(pl.BlockSp...]
where the time goes in v1:
time: 35.3 us; the launch traced here: 35.1 us
  Pallas kernels  13.8 us (39%)
  starting transfers between devices  9.87 us (28%)
  waiting for transfers between devices  8.96 us (25%)
  local copies, waits for them, and re-layouts  1.36 us (4%)
  between operations  0.68 us (2%)
  other arithmetic  0.43 us (1%)
    pallas_call x1, Pallas kernels, finish(): pl.pallas_call(finish_kernel, in_specs=[whole] * 4, out_specs=(pl.BlockSp...  11.7 us
    ppermute x4, starting transfers between devices, sum_over(): block = block + lax.ppermute(block, (core_axis, axis), route)  8.76 us
    ppermute x4, waiting for transfers between devices, sum_over(): block = block + lax.ppermute(block, (core_axis, axis), route)  8.23 us
    unnamed x3, local copies, waits for them, and re-layouts  1.29 us
    pallas_call x1, Pallas kernels, packed_grams(): pl.pallas_call(pack_kernel, in_specs=[whole] * 3, out_specs=whole, out_sh...  1.11 us
    pallas_call x1, Pallas kernels, packed_grams(): pl.pallas_call(own_gram_kernel, in_specs=[whole], out_specs=(whole, whole...  1.05 us
  transfers between devices with their start and end apart: 6, of which 6 were waited for; matrix products, arithmetic and copies ran while one was open for 1% of the time, Pallas kernels for 3%

profile of v1, /device:TPU:0, one launch (start us, length us, event | category | flops | bytes accessed | tf_op | source)
XLA Modules:
  0.0 35.1 jit_solution(8133996355198242509)
XLA Ops:
  0.6 0.6 %collective-permute-start = (f32[128,2048]{1,0:T(8,128)}, f32[128,2048]{1,0:T(8,128)S(1)}, u32[]{:S(2)}, u32[]{:S(2)}) collective-permute-start(f32[128,2048]{1,0:T(8,128)} %own_ref.1), channel_id=1, source_target_pairs={{0,16},{16,0},{1,17},{17,1},{2,18},{18,2},{3,19},{19,3},{4,20},{20... | collective-permute-start | bytes 3145736 | tf_op jit(solution)/shard_map/ppermute | solution.py:248
  1.2 0.0 copy-start
  1.2 1.2 %copy-done = f32[128,2048]{1,0:T(8,128)S(1)} copy-done((f32[128,2048]{1,0:T(8,128)S(1)}, f32[128,2048]{1,0:T(8,128)}, u32[]{:S(2)}) %copy-start) | copy-done | bytes 1048600
  2.4 1.1 %shard_map.30 = (f32[128,128]{1,0:T(8,128)S(1)}, f32[128,2048]{1,0:T(8,128)S(1)}) custom-call(f32[128,2048]{1,0:T(8,128)S(1)} %copy-done), custom_call_target="tpu_custom_call" | custom-call | flops 402653184 | bytes 1048576 | tf_op jit(solution)/shard_map/pallas_call | solution.py:190
  3.5 0.2 collective-permute-done.other_ref
  3.7 1.1 %shard_map.31 = f32[136,128]{1,0:T(8,128)S(1)} custom-call(f32[128,2048]{1,0:T(8,128)S(1)} %get-tuple-element.4.own_ref, f32[128,2048]{1,0:T(8,128)S(1)} %collective-permute-done.other_ref, f32[128,128]{1,0:T(8,128)S(1)} %get-tuple-element.5.own_gram_ref), custom_call_target="tpu_custom_call" | custom-call | flops 402653184 | bytes 2097152 | tf_op jit(solution)/shard_map/pallas_call | solution.py:198
  4.8 3.8 %collective-permute-start.1 = (f32[136,128]{1,0:T(8,128)S(1)}, f32[136,128]{1,0:T(8,128)S(1)}, u32[]{:S(2)}, u32[]{:S(2)}) collective-permute-start(f32[136,128]{1,0:T(8,128)S(1)} %shard_map.31), channel_id=1, source_target_pairs={{0,24},{1,16},{2,19},{3,27},{4,21},{5,29},{6,30},{7,22},{8,25},{9,... | collective-permute-start | bytes 208904 | tf_op jit(solution)/shard_map/ppermute | solution.py:40
  8.6 2.0 %collective-permute-done.1 = f32[136,128]{1,0:T(8,128)S(1)} collective-permute-done((f32[136,128]{1,0:T(8,128)S(1)}, f32[136,128]{1,0:T(8,128)S(1)}, u32[]{:S(2)}, u32[]{:S(2)}) %collective-permute-start.1) | collective-permute-done | bytes 69664 | tf_op jit(solution)/shard_map/ppermute | solution.py:40
  10.6 1.6 %collective-permute-start.2 = (f32[136,128]{1,0:T(8,128)S(1)}, f32[136,128]{1,0:T(8,128)S(1)}, u32[]{:S(2)}, u32[]{:S(2)}) collective-permute-start(f32[136,128]{1,0:T(8,128)S(1)} %add.12), channel_id=1, source_target_pairs={{0,17},{1,25},{2,26},{3,18},{4,28},{5,20},{6,23},{7,31},{8,16},{9,... | collective-permute-start | bytes 208904 | tf_op jit(solution)/shard_map/ppermute | solution.py:40
  12.2 2.2 %collective-permute-done.2 = f32[136,128]{1,0:T(8,128)S(1)} collective-permute-done((f32[136,128]{1,0:T(8,128)S(1)}, f32[136,128]{1,0:T(8,128)S(1)}, u32[]{:S(2)}, u32[]{:S(2)}) %collective-permute-start.2) | collective-permute-done | bytes 69664 | tf_op jit(solution)/shard_map/ppermute | solution.py:40
  14.4 1.6 %collective-permute-start.3 = (f32[136,128]{1,0:T(8,128)S(1)}, f32[136,128]{1,0:T(8,128)S(1)}, u32[]{:S(2)}, u32[]{:S(2)}) collective-permute-start(f32[136,128]{1,0:T(8,128)S(1)} %add.13), channel_id=1, source_target_pairs={{0,18},{1,21},{2,22},{3,17},{4,16},{5,23},{6,20},{7,19},{8,28},{9,... | collective-permute-start | bytes 208904 | tf_op jit(solution)/shard_map/ppermute | solution.py:40
  16.0 0.1 constant_dynamic-update-slice_fusion.1
  16.1 2.1 %collective-permute-done.3 = f32[136,128]{1,0:T(8,128)S(1)} collective-permute-done((f32[136,128]{1,0:T(8,128)S(1)}, f32[136,128]{1,0:T(8,128)S(1)}, u32[]{:S(2)}, u32[]{:S(2)}) %collective-permute-start.3) | collective-permute-done | bytes 69664 | tf_op jit(solution)/shard_map/ppermute | solution.py:40
  18.2 1.7 %collective-permute-start.4 = (f32[136,128]{1,0:T(8,128)S(1)}, f32[136,128]{1,0:T(8,128)S(1)}, u32[]{:S(2)}, u32[]{:S(2)}) collective-permute-start(f32[136,128]{1,0:T(8,128)S(1)} %add.14), channel_id=1, source_target_pairs={{0,20},{1,19},{2,16},{3,23},{4,22},{5,17},{6,18},{7,21},{8,26},{9,... | collective-permute-start | bytes 208904 | tf_op jit(solution)/shard_map/ppermute | solution.py:40
  19.9 0.1 constant_dynamic-update-slice_fusion
  20.0 2.0 %collective-permute-done.4 = f32[136,128]{1,0:T(8,128)S(1)} collective-permute-done((f32[136,128]{1,0:T(8,128)S(1)}, f32[136,128]{1,0:T(8,128)S(1)}, u32[]{:S(2)}, u32[]{:S(2)}) %collective-permute-start.4) | collective-permute-done | bytes 69664 | tf_op jit(solution)/shard_map/ppermute | solution.py:40
  22.0 0.5 %collective-permute-start.5 = (f32[136,128]{1,0:T(8,128)S(1)}, f32[136,128]{1,0:T(8,128)S(1)}, u32[]{:S(2)}, u32[]{:S(2)}) collective-permute-start(f32[136,128]{1,0:T(8,128)S(1)} %add.15.summed_ref), channel_id=1, source_target_pairs={{0,16},{16,0},{1,17},{17,1},{2,18},{18,2},{3,19},{19,3},{4,20},{20... | collective-permute-start | bytes 208904 | tf_op jit(solution)/shard_map/ppermute | solution.py:251
  22.5 0.4 %fusion = (bf16[256,2048]{1,0:T(8,128)(2,1)S(1)}, bf16[256,2048]{1,0:T(8,128)(2,1)S(1)}) fusion(f32[256,2048]{1,0:T(8,128)S(1)} %constant_dynamic-update-slice_fusion), kind=kLoop, calls=%fused_computation.2 | loop fusion | flops 2097152 | bytes 4194304 | tf_op jit(solution)/shard_map/convert_element_type | solution.py:254
  22.9 0.5 %collective-permute-done.5.given_ref = f32[136,128]{1,0:T(8,128)S(1)} collective-permute-done((f32[136,128]{1,0:T(8,128)S(1)}, f32[136,128]{1,0:T(8,128)S(1)}, u32[]{:S(2)}, u32[]{:S(2)}) %collective-permute-start.5) | collective-permute-done | bytes 69664 | tf_op jit(solution)/shard_map/ppermute | solution.py:251
  23.5 11.7 %shard_map.32 = (f32[128,2048]{1,0:T(8,128)}, f32[128,2048]{1,0:T(8,128)}) custom-call(f32[136,128]{1,0:T(8,128)S(1)} %add.15.summed_ref, f32[136,128]{1,0:T(8,128)S(1)} %collective-permute-done.5.given_ref, bf16[256,2048]{1,0:T(8,128)(2,1)S(1)} %get-tuple-element.7.high_ref, bf16[256,2048]{1,0:T(8,128)(2,1)S(1)} %get-tuple-element.6.low_ref), custom_call_target="tpu_custom_call" | custom-call | tf_op jit(solution)/shard_map/pallas_call | solution.py:237
  (4 shorter events, 0.0 us)
Async XLA Ops:
  0.6 3.1 %collective-permute-start = (f32[128,2048]{1,0:T(8,128)}, f32[128,2048]{1,0:T(8,128)S(1)}, u32[]{:S(2)}, u32[]{:S(2)}) collective-permute-start(f32[128,2048]{1,0:T(8,128)} %own_ref.1), channel_id=1, source_target_pairs={{0,16},{16,0},{1,17},{17,1},{2,18},{18,2},{3,19},{19,3},{4,20},{20... | collective-permute-start | bytes 3145736 | tf_op jit(solution)/shard_map/ppermute | solution.py:248
  1.2 1.2 %copy-start = (f32[128,2048]{1,0:T(8,128)S(1)}, f32[128,2048]{1,0:T(8,128)}, u32[]{:S(2)}) copy-start(f32[128,2048]{1,0:T(8,128)} %own_ref.1) | copy-start | bytes 3145732
  4.8 5.7 %collective-permute-start.1 = (f32[136,128]{1,0:T(8,128)S(1)}, f32[136,128]{1,0:T(8,128)S(1)}, u32[]{:S(2)}, u32[]{:S(2)}) collective-permute-start(f32[136,128]{1,0:T(8,128)S(1)} %shard_map.31), channel_id=1, source_target_pairs={{0,24},{1,16},{2,19},{3,27},{4,21},{5,29},{6,30},{7,22},{8,25},{9,... | collective-permute-start | bytes 208904 | tf_op jit(solution)/shard_map/ppermute | solution.py:40
  10.6 3.8 %collective-permute-start.2 = (f32[136,128]{1,0:T(8,128)S(1)}, f32[136,128]{1,0:T(8,128)S(1)}, u32[]{:S(2)}, u32[]{:S(2)}) collective-permute-start(f32[136,128]{1,0:T(8,128)S(1)} %add.12), channel_id=1, source_target_pairs={{0,17},{1,25},{2,26},{3,18},{4,28},{5,20},{6,23},{7,31},{8,16},{9,... | collective-permute-start | bytes 208904 | tf_op jit(solution)/shard_map/ppermute | solution.py:40
  14.4 3.8 %collective-permute-start.3 = (f32[136,128]{1,0:T(8,128)S(1)}, f32[136,128]{1,0:T(8,128)S(1)}, u32[]{:S(2)}, u32[]{:S(2)}) collective-permute-start(f32[136,128]{1,0:T(8,128)S(1)} %add.13), channel_id=1, source_target_pairs={{0,18},{1,21},{2,22},{3,17},{4,16},{5,23},{6,20},{7,19},{8,28},{9,... | collective-permute-start | bytes 208904 | tf_op jit(solution)/shard_map/ppermute | solution.py:40
  18.2 3.8 %collective-permute-start.4 = (f32[136,128]{1,0:T(8,128)S(1)}, f32[136,128]{1,0:T(8,128)S(1)}, u32[]{:S(2)}, u32[]{:S(2)}) collective-permute-start(f32[136,128]{1,0:T(8,128)S(1)} %add.14), channel_id=1, source_target_pairs={{0,20},{1,19},{2,16},{3,23},{4,22},{5,17},{6,18},{7,21},{8,26},{9,... | collective-permute-start | bytes 208904 | tf_op jit(solution)/shard_map/ppermute | solution.py:40
  22.0 1.5 %collective-permute-start.5 = (f32[136,128]{1,0:T(8,128)S(1)}, f32[136,128]{1,0:T(8,128)S(1)}, u32[]{:S(2)}, u32[]{:S(2)}) collective-permute-start(f32[136,128]{1,0:T(8,128)S(1)} %add.15.summed_ref), channel_id=1, source_target_pairs={{0,16},{16,0},{1,17},{17,1},{2,18},{18,2},{3,19},{19,3},{4,20},{20... | collective-permute-start | bytes 208904 | tf_op jit(solution)/shard_map/ppermute | solution.py:251

commit v2 on v1

--- a/solution.py
+++ b/solution.py
@@ -14,6 +14,33 @@
 
 def nt(left, right):
     return lax.dot_general(left, right, (((1,), (1,)), ((), ())), precision=lax.Precision.HIGHEST, preferred_element_type=jnp.float32)
+
+
+def split(block):
+    high = block.astype(jnp.bfloat16)
+    return high, (block - high.astype(jnp.float32)).astype(jnp.bfloat16)
+
+
+def parts(block, axis):
+    return jnp.concatenate(split(block), axis=axis)
+
+
+def corners(block):
+    rows, columns = block.shape[0] // 2, block.shape[1] // 2
+    top, bottom = block[:rows], block[rows:]
+    return top[:, :columns] + (top[:, columns:] + bottom[:, :columns] + bottom[:, columns:])
+
+
+def nn_parts(left, right):
+    return corners(jnp.dot(parts(left, 0), parts(right, 1), preferred_element_type=jnp.float32))
+
+
+def nt_high_low(left, right):
+    return corners(lax.dot_general(left, right, (((1,), (1,)), ((), ())), preferred_element_type=jnp.float32))
+
+
+def nt_parts(left, right):
+    return nt_high_low(parts(left, 0), parts(right, 0))
 
 
 def parity(index):
@@ -121,17 +148,12 @@
     root, damped = inverse_factors([reduced, reduced + jnp.where(on_diagonal, delta, 0.0)], 8, 4)
     shrunk = nt(reduced, damped)
     whitened = nn(root, basis[0]), nn(root, basis[1])
-    mixing = nn(shrunk, whitened[0]), nn(shrunk, whitened[1])
-    left = jnp.where(is_upper, cross.T, lower_gram)
-    right = jnp.where(is_upper, upper_gram, cross)
+    whitened = jnp.concatenate(whitened, axis=1)
+    mixing = nn_parts(shrunk, whitened)
+    own_rows = jnp.concatenate([jnp.where(is_upper, cross.T, lower_gram), jnp.where(is_upper, upper_gram, cross)], axis=1)
     scaling = 4.0 * kept / (total(shrunk * shrunk) + 1e-06)
-    coeffs = nt(nt(left, whitened[0]) + nt(right, whitened[1]), shrunk) * scaling
+    coeffs = nt_parts(nt_parts(own_rows, whitened), shrunk) * scaling
     return mixing, coeffs
-
-
-def split(block):
-    high = block.astype(jnp.bfloat16)
-    return high, (block - high.astype(jnp.float32)).astype(jnp.bfloat16)
 
 
 def stacked(block):
@@ -150,20 +172,21 @@
     return (lax.broadcasted_iota(jnp.int32, (size, size), axis) for axis in (0, 1))
 
 
-def own_gram_kernel(own_ref, gram_ref, kept_ref):
-    own = own_ref[...]
-    kept_ref[...] = own
-    gram_ref[...] = nt(own, own)
-
-
-def pack_kernel(own_ref, other_ref, own_gram_ref, packed_ref):
-    kept = own_ref.shape[0]
+def own_gram_kernel(own_ref, gram_ref, parts_ref):
+    own = parts(own_ref[...], 0)
+    parts_ref[...] = own
+    gram_ref[...] = nt_high_low(own, own)
+
+
+def pack_kernel(own_ref, other_ref, own_gram_ref, packed_ref, parts_ref):
+    kept = other_ref.shape[0]
     is_upper = lax.axis_index("frames") == 1
     is_cross = half_of("frames", "pix") == 0
-    own, other = own_ref[...], other_ref[...]
+    own, other = own_ref[...], parts(other_ref[...], 0)
+    parts_ref[...] = other
     left = jnp.where(is_cross & ~is_upper, own, other)
     right = jnp.where(is_cross & is_upper, own, other)
-    fresh = nt(left, right)
+    fresh = nt_high_low(left, right)
     row, column = positions(kept)
     own_gram = own_gram_ref[...]
     upper_gram = jnp.where(is_upper, own_gram, fresh)
@@ -187,39 +210,44 @@
     kept, width = own.shape
     whole = pl.BlockSpec(memory_space=pltpu.VMEM)
     grant = pltpu.CompilerParams(vmem_limit_bytes=16 << 20)
+    cost = pl.CostEstimate(flops=12 * kept * kept * width, bytes_accessed=8 * kept * width, transcendentals=0)
+    both = jax.ShapeDtypeStruct((2 * kept, width), jnp.bfloat16)
     own_gram, own = pl.pallas_call(
         own_gram_kernel,
         in_specs=[whole],
         out_specs=(whole, whole),
-        out_shape=(jax.ShapeDtypeStruct((kept, kept), jnp.float32), jax.ShapeDtypeStruct((kept, width), jnp.float32)),
+        out_shape=(jax.ShapeDtypeStruct((kept, kept), jnp.float32), both),
         compiler_params=grant,
-        cost_estimate=pl.CostEstimate(flops=12 * kept * kept * width, bytes_accessed=4 * kept * width, transcendentals=0),
+        cost_estimate=cost,
     )(own)
-    packed = pl.pallas_call(
+    packed, other = pl.pallas_call(
         pack_kernel,
         in_specs=[whole] * 3,
-        out_specs=whole,
-        out_shape=jax.ShapeDtypeStruct((kept + 8, kept), jnp.float32),
+        out_specs=(whole, whole),
+        out_shape=(jax.ShapeDtypeStruct((kept + 8, kept), jnp.float32), both),
         compiler_params=grant,
-        cost_estimate=pl.CostEstimate(flops=12 * kept * kept * width, bytes_accessed=8 * kept * width, transcendentals=0),
+        cost_estimate=cost,
     )(own, other, own_gram)
-    return packed, own
-
-
-def finish_kernel(summed_ref, given_ref, high_ref, low_ref, sketch_ref, projected_ref, sketch_buf, projected_buf, sems):
+    return packed, own, other
+
+
+def finish_kernel(summed_ref, given_ref, own_ref, other_ref, sketch_ref, projected_ref, sketch_buf, projected_buf, sems):
     kept, width = sketch_buf.shape
     is_upper = lax.axis_index("frames") == 1
     has_cross = half_of("frames", "pix") == 0
     cross = jnp.where(has_cross, summed_ref[:kept], given_ref[:kept])
     lower_gram, upper_gram = unpack(jnp.where(has_cross, given_ref[...], summed_ref[...]))
-    (first, second), coeffs = transform(lower_gram, cross, upper_gram, is_upper)
+    mixing, coeffs = transform(lower_gram, cross, upper_gram, is_upper)
+    first, second = mixing[:, :kept], mixing[:, kept:]
     mixing = stacked(jnp.concatenate([jnp.where(is_upper, second, first), jnp.where(is_upper, first, second)], axis=1))
     coeffs = stacked(coeffs)
     block = min(width, 512)
     copies = []
     for k in range(width // block):
         columns = pl.ds(k * block, block)
-        sketch = product(mixing, high_ref[:, columns], low_ref[:, columns])
+        high = jnp.concatenate([own_ref[:kept, columns], other_ref[:kept, columns]], axis=0)
+        low = jnp.concatenate([own_ref[kept:, columns], other_ref[kept:, columns]], axis=0)
+        sketch = product(mixing, high, low)
         sketch_buf[:, columns] = sketch
         copies.append(pltpu.make_async_copy(sketch_buf.at[:, columns], sketch_ref.at[:, columns], sems.at[2 * k]))
         copies[-1].start()
@@ -230,9 +258,8 @@
         copy.wait()
 
 
-def finish(summed, given, high, low):
-    width = high.shape[1]
-    kept = high.shape[0] // 2
+def finish(summed, given, own, other):
+    kept, width = own.shape[0] // 2, own.shape[1]
     whole = pl.BlockSpec(memory_space=pltpu.VMEM)
     return pl.pallas_call(
         finish_kernel,
@@ -241,18 +268,15 @@
         out_shape=(jax.ShapeDtypeStruct((kept, width), jnp.float32),) * 2,
         scratch_shapes=[pltpu.VMEM((kept, width), jnp.float32)] * 2 + [pltpu.SemaphoreType.DMA((2 * max(1, width // 512),))],
         compiler_params=pltpu.CompilerParams(vmem_limit_bytes=24 << 20),
-    )(summed, given, high, low)
+    )(summed, given, own, other)
 
 
 def local(frames):
     other = lax.ppermute(frames, "frames", [(0, 1), (1, 0)])
-    packed, own = packed_grams(frames, other)
+    packed, own, other = packed_grams(frames, other)
     summed = sum_over(packed, "pix", "frames")
     given = lax.ppermute(summed, "frames", [(0, 1), (1, 0)])
-    rows = jnp.concatenate([own, other], axis=0)
-    high = lax.reduce_precision(rows, 8, 7)
-    low = (rows - high).astype(jnp.bfloat16)
-    return finish(summed, given, high.astype(jnp.bfloat16), low)
+    return finish(summed, given, own, other)
 
 
 def solution(mesh):

time: 35.3 us -> 34.2 us (0.969)
  Pallas kernels: 13.8 us -> 12.2 us
  waiting for transfers between devices: 8.96 us -> 10 us
  other arithmetic: 0.43 us -> 0.04 us
    pallas_call x1, Pallas kernels: 11.7 us -> 11 us  [finish(): pl.pallas_call(finish_kernel, in_specs=[whole] * 4, out_specs=(pl.BlockSp...]
    ppermute x1, waiting for transfers between devices: 0.21 us -> 0.74 us  [local(): other = lax.ppermute(frames, 'frames', [(0, 1), (1, 0)])]
    pallas_call x1, Pallas kernels: 1.05 us -> 0.52 us  [packed_grams(): pl.pallas_call(own_gram_kernel, in_specs=[whole], out_specs=(whole, whole...]
    pallas_call x1, Pallas kernels: 1.11 us -> 0.63 us  [packed_grams(): pl.pallas_call(pack_kernel, in_specs=[whole] * 3, out_specs=(whole, whole...]
    ppermute x1, waiting for transfers between devices: 0.51 us -> 0.91 us  [local(): given = lax.ppermute(summed, 'frames', [(0, 1), (1, 0)])]
    convert_element_type x1 -> x0, other arithmetic: 0.39 us -> none  [local(): low = (rows - high).astype(jnp.bfloat16)]
    unnamed x3 -> x2, local copies, waits for them, and re-layouts: 1.29 us -> 1.22 us
  transfers between devices with their start and end apart: 6 -> 6, of which waited for: 6 -> 6; matrix products, arithmetic and copies ran while one was open for 1% -> 0% of each run, Pallas kernels for 3% -> 2%
where the time goes in v2:
time: 34.2 us; the launch traced here: 34 us
  Pallas kernels  12.2 us (36%)
  waiting for transfers between devices  10 us (29%)
  starting transfers between devices  9.87 us (29%)
  local copies, waits for them, and re-layouts  1.22 us (4%)
  between operations  0.66 us (2%)
    pallas_call x1, Pallas kernels, finish(): pl.pallas_call(finish_kernel, in_specs=[whole] * 4, out_specs=(pl.BlockSp...  11 us
    ppermute x4, starting transfers between devices, sum_over(): block = block + lax.ppermute(block, (core_axis, axis), route)  8.76 us
    ppermute x4, waiting for transfers between devices, sum_over(): block = block + lax.ppermute(block, (core_axis, axis), route)  8.38 us
    unnamed x2, local copies, waits for them, and re-layouts  1.22 us
    ppermute x1, waiting for transfers between devices, local(): given = lax.ppermute(summed, 'frames', [(0, 1), (1, 0)])  0.91 us
    ppermute x1, waiting for transfers between devices, local(): other = lax.ppermute(frames, 'frames', [(0, 1), (1, 0)])  0.74 us
  transfers between devices with their start and end apart: 6, of which 6 were waited for; matrix products, arithmetic and copies ran while one was open for 0% of the time, Pallas kernels for 2%

profile of v2, /device:TPU:0, one launch (start us, length us, event | category | flops | bytes accessed | tf_op | source)
XLA Modules:
  0.0 34.0 jit_solution(11922083841992682411)
XLA Ops:
  0.6 0.6 %collective-permute-start = (f32[128,2048]{1,0:T(8,128)}, f32[128,2048]{1,0:T(8,128)S(1)}, u32[]{:S(2)}, u32[]{:S(2)}) collective-permute-start(f32[128,2048]{1,0:T(8,128)} %own_ref.1), channel_id=1, source_target_pairs={{0,16},{16,0},{1,17},{17,1},{2,18},{18,2},{3,19},{19,3},{4,20},{20... | collective-permute-start | bytes 3145736 | tf_op jit(solution)/shard_map/ppermute | solution.py:275
  1.2 0.0 copy-start
  1.2 1.2 %copy-done = f32[128,2048]{1,0:T(8,128)S(1)} copy-done((f32[128,2048]{1,0:T(8,128)S(1)}, f32[128,2048]{1,0:T(8,128)}, u32[]{:S(2)}) %copy-start) | copy-done | bytes 1048600
  2.4 0.5 %shard_map.30 = (f32[128,128]{1,0:T(8,128)S(1)}, bf16[256,2048]{1,0:T(8,128)(2,1)S(1)}) custom-call(f32[128,2048]{1,0:T(8,128)S(1)} %copy-done), custom_call_target="tpu_custom_call" | custom-call | flops 402653184 | bytes 2097152 | tf_op jit(solution)/shard_map/pallas_call | solution.py:215
  2.9 0.7 %collective-permute-done.other_ref = f32[128,2048]{1,0:T(8,128)S(1)} collective-permute-done((f32[128,2048]{1,0:T(8,128)}, f32[128,2048]{1,0:T(8,128)S(1)}, u32[]{:S(2)}, u32[]{:S(2)}) %collective-permute-start) | collective-permute-done | bytes 1048608 | tf_op jit(solution)/shard_map/ppermute | solution.py:275
  3.7 0.6 %shard_map.31 = (f32[136,128]{1,0:T(8,128)S(1)}, bf16[256,2048]{1,0:T(8,128)(2,1)S(1)}) custom-call(bf16[256,2048]{1,0:T(8,128)(2,1)S(1)} %get-tuple-element.6.own_ref, f32[128,2048]{1,0:T(8,128)S(1)} %collective-permute-done.other_ref, f32[128,128]{1,0:T(8,128)S(1)} %get-tuple-element.7.own_gram_ref), custom_call_target="tpu_custom_call" | custom-call | flops 402653184 | bytes 2097152 | tf_op jit(solution)/shard_map/pallas_call | solution.py:223
  4.3 3.8 %collective-permute-start.1 = (f32[136,128]{1,0:T(8,128)S(1)}, f32[136,128]{1,0:T(8,128)S(1)}, u32[]{:S(2)}, u32[]{:S(2)}) collective-permute-start(f32[136,128]{1,0:T(8,128)S(1)} %get-tuple-element.8), channel_id=1, source_target_pairs={{0,24},{1,16},{2,19},{3,27},{4,21},{5,29},{6,30},{7,22},{8,25},{9,... | collective-permute-start | bytes 208904 | tf_op jit(solution)/shard_map/ppermute | solution.py:67
  8.1 2.0 %collective-permute-done.1 = f32[136,128]{1,0:T(8,128)S(1)} collective-permute-done((f32[136,128]{1,0:T(8,128)S(1)}, f32[136,128]{1,0:T(8,128)S(1)}, u32[]{:S(2)}, u32[]{:S(2)}) %collective-permute-start.1) | collective-permute-done | bytes 69664 | tf_op jit(solution)/shard_map/ppermute | solution.py:67
  10.1 1.6 %collective-permute-start.2 = (f32[136,128]{1,0:T(8,128)S(1)}, f32[136,128]{1,0:T(8,128)S(1)}, u32[]{:S(2)}, u32[]{:S(2)}) collective-permute-start(f32[136,128]{1,0:T(8,128)S(1)} %add.12), channel_id=1, source_target_pairs={{0,17},{1,25},{2,26},{3,18},{4,28},{5,20},{6,23},{7,31},{8,16},{9,... | collective-permute-start | bytes 208904 | tf_op jit(solution)/shard_map/ppermute | solution.py:67
  11.7 2.2 %collective-permute-done.2 = f32[136,128]{1,0:T(8,128)S(1)} collective-permute-done((f32[136,128]{1,0:T(8,128)S(1)}, f32[136,128]{1,0:T(8,128)S(1)}, u32[]{:S(2)}, u32[]{:S(2)}) %collective-permute-start.2) | collective-permute-done | bytes 69664 | tf_op jit(solution)/shard_map/ppermute | solution.py:67
  13.9 1.6 %collective-permute-start.3 = (f32[136,128]{1,0:T(8,128)S(1)}, f32[136,128]{1,0:T(8,128)S(1)}, u32[]{:S(2)}, u32[]{:S(2)}) collective-permute-start(f32[136,128]{1,0:T(8,128)S(1)} %add.13), channel_id=1, source_target_pairs={{0,18},{1,21},{2,22},{3,17},{4,16},{5,23},{6,20},{7,19},{8,28},{9,... | collective-permute-start | bytes 208904 | tf_op jit(solution)/shard_map/ppermute | solution.py:67
  15.5 2.2 %collective-permute-done.3 = f32[136,128]{1,0:T(8,128)S(1)} collective-permute-done((f32[136,128]{1,0:T(8,128)S(1)}, f32[136,128]{1,0:T(8,128)S(1)}, u32[]{:S(2)}, u32[]{:S(2)}) %collective-permute-start.3) | collective-permute-done | bytes 69664 | tf_op jit(solution)/shard_map/ppermute | solution.py:67
  17.7 1.7 %collective-permute-start.4 = (f32[136,128]{1,0:T(8,128)S(1)}, f32[136,128]{1,0:T(8,128)S(1)}, u32[]{:S(2)}, u32[]{:S(2)}) collective-permute-start(f32[136,128]{1,0:T(8,128)S(1)} %add.14), channel_id=1, source_target_pairs={{0,20},{1,19},{2,16},{3,23},{4,22},{5,17},{6,18},{7,21},{8,26},{9,... | collective-permute-start | bytes 208904 | tf_op jit(solution)/shard_map/ppermute | solution.py:67
  19.5 2.1 %collective-permute-done.4 = f32[136,128]{1,0:T(8,128)S(1)} collective-permute-done((f32[136,128]{1,0:T(8,128)S(1)}, f32[136,128]{1,0:T(8,128)S(1)}, u32[]{:S(2)}, u32[]{:S(2)}) %collective-permute-start.4) | collective-permute-done | bytes 69664 | tf_op jit(solution)/shard_map/ppermute | solution.py:67
  21.5 0.5 %collective-permute-start.5 = (f32[136,128]{1,0:T(8,128)S(1)}, f32[136,128]{1,0:T(8,128)S(1)}, u32[]{:S(2)}, u32[]{:S(2)}) collective-permute-start(f32[136,128]{1,0:T(8,128)S(1)} %add.15.summed_ref), channel_id=1, source_target_pairs={{0,16},{16,0},{1,17},{17,1},{2,18},{18,2},{3,19},{19,3},{4,20},{20... | collective-permute-start | bytes 208904 | tf_op jit(solution)/shard_map/ppermute | solution.py:278
  22.1 0.9 %collective-permute-done.5.given_ref = f32[136,128]{1,0:T(8,128)S(1)} collective-permute-done((f32[136,128]{1,0:T(8,128)S(1)}, f32[136,128]{1,0:T(8,128)S(1)}, u32[]{:S(2)}, u32[]{:S(2)}) %collective-permute-start.5) | collective-permute-done | bytes 69664 | tf_op jit(solution)/shard_map/ppermute | solution.py:278
  23.0 11.0 %shard_map.32 = (f32[128,2048]{1,0:T(8,128)}, f32[128,2048]{1,0:T(8,128)}) custom-call(f32[136,128]{1,0:T(8,128)S(1)} %add.15.summed_ref, f32[136,128]{1,0:T(8,128)S(1)} %collective-permute-done.5.given_ref, bf16[256,2048]{1,0:T(8,128)(2,1)S(1)} %get-tuple-element.6.own_ref, bf16[256,2048]{1,0:T(8,128)(2,1)S(1)} %get-tuple-element.9.other_ref), custom_call_target="tpu_custom_call" | custom-call | tf_op jit(solution)/shard_map/pallas_call | solution.py:264
  (4 shorter events, 0.0 us)
Async XLA Ops:
  0.6 3.1 %collective-permute-start = (f32[128,2048]{1,0:T(8,128)}, f32[128,2048]{1,0:T(8,128)S(1)}, u32[]{:S(2)}, u32[]{:S(2)}) collective-permute-start(f32[128,2048]{1,0:T(8,128)} %own_ref.1), channel_id=1, source_target_pairs={{0,16},{16,0},{1,17},{17,1},{2,18},{18,2},{3,19},{19,3},{4,20},{20... | collective-permute-start | bytes 3145736 | tf_op jit(solution)/shard_map/ppermute | solution.py:275
  1.2 1.2 %copy-start = (f32[128,2048]{1,0:T(8,128)S(1)}, f32[128,2048]{1,0:T(8,128)}, u32[]{:S(2)}) copy-start(f32[128,2048]{1,0:T(8,128)} %own_ref.1) | copy-start | bytes 3145732
  4.3 5.7 %collective-permute-start.1 = (f32[136,128]{1,0:T(8,128)S(1)}, f32[136,128]{1,0:T(8,128)S(1)}, u32[]{:S(2)}, u32[]{:S(2)}) collective-permute-start(f32[136,128]{1,0:T(8,128)S(1)} %get-tuple-element.8), channel_id=1, source_target_pairs={{0,24},{1,16},{2,19},{3,27},{4,21},{5,29},{6,30},{7,22},{8,25},{9,... | collective-permute-start | bytes 208904 | tf_op jit(solution)/shard_map/ppermute | solution.py:67
  10.1 3.8 %collective-permute-start.2 = (f32[136,128]{1,0:T(8,128)S(1)}, f32[136,128]{1,0:T(8,128)S(1)}, u32[]{:S(2)}, u32[]{:S(2)}) collective-permute-start(f32[136,128]{1,0:T(8,128)S(1)} %add.12), channel_id=1, source_target_pairs={{0,17},{1,25},{2,26},{3,18},{4,28},{5,20},{6,23},{7,31},{8,16},{9,... | collective-permute-start | bytes 208904 | tf_op jit(solution)/shard_map/ppermute | solution.py:67
  13.9 3.8 %collective-permute-start.3 = (f32[136,128]{1,0:T(8,128)S(1)}, f32[136,128]{1,0:T(8,128)S(1)}, u32[]{:S(2)}, u32[]{:S(2)}) collective-permute-start(f32[136,128]{1,0:T(8,128)S(1)} %add.13), channel_id=1, source_target_pairs={{0,18},{1,21},{2,22},{3,17},{4,16},{5,23},{6,20},{7,19},{8,28},{9,... | collective-permute-start | bytes 208904 | tf_op jit(solution)/shard_map/ppermute | solution.py:67
  17.7 3.8 %collective-permute-start.4 = (f32[136,128]{1,0:T(8,128)S(1)}, f32[136,128]{1,0:T(8,128)S(1)}, u32[]{:S(2)}, u32[]{:S(2)}) collective-permute-start(f32[136,128]{1,0:T(8,128)S(1)} %add.14), channel_id=1, source_target_pairs={{0,20},{1,19},{2,16},{3,23},{4,22},{5,17},{6,18},{7,21},{8,26},{9,... | collective-permute-start | bytes 208904 | tf_op jit(solution)/shard_map/ppermute | solution.py:67
  21.5 1.5 %collective-permute-start.5 = (f32[136,128]{1,0:T(8,128)S(1)}, f32[136,128]{1,0:T(8,128)S(1)}, u32[]{:S(2)}, u32[]{:S(2)}) collective-permute-start(f32[136,128]{1,0:T(8,128)S(1)} %add.15.summed_ref), channel_id=1, source_target_pairs={{0,16},{16,0},{1,17},{17,1},{2,18},{18,2},{3,19},{19,3},{4,20},{20... | collective-permute-start | bytes 208904 | tf_op jit(solution)/shard_map/ppermute | solution.py:278

commit v3 on v2

--- a/solution.py
+++ b/solution.py
@@ -4,9 +4,6 @@
 from jax.experimental import pallas as pl
 from jax.experimental.pallas import tpu as pltpu
 from jax.sharding import PartitionSpec as P
-
-PANEL = 32
-
 
 def nn(left, right):
     return lax.dot_general(left, right, (((1,), (0,)), ((), ())), precision=lax.Precision.HIGHEST, preferred_element_type=jnp.float32)
@@ -106,15 +103,15 @@
     return carried
 
 
-def inverse_factors(grams, group, ahead):
+def inverse_factors(grams, panel, group, ahead):
     size = grams[0].shape[0]
-    count, step = size // 8, PANEL // 8
+    count, step = size // 8, panel // 8
     column = lax.broadcasted_iota(jnp.int32, (8, size), 1)
     sub = lax.broadcasted_iota(jnp.int32, (8, size), 0)
     left = [[gram[8 * i : 8 * i + 8] for i in range(count)] for gram in grams]
     right = [[(column == sub + 8 * i).astype(jnp.float32) for i in range(count)] for _ in grams]
     for first in range(0, count, step):
-        rest = first + step
+        rest = min(first + step, count)
         for a, z in zip(left, right):
             block = a[first:rest]
             if rest == count:
@@ -137,18 +134,18 @@
 
 def transform(lower_gram, cross, upper_gram, is_upper):
     kept = lower_gram.shape[0]
-    normal = nt(lower_gram, lower_gram) + nt(cross, cross)
-    beside = nn(lower_gram, cross) + nn(cross, upper_gram)
-    (inverse,) = inverse_factors([normal], 16, 6)
-    basis = nn(inverse, lower_gram), nn(inverse, cross)
-    image = nn(inverse, normal), nn(inverse, beside)
-    reduced = nt(image[0], basis[0]) + nt(image[1], basis[1])
-    delta = total(image[0] * basis[0] + image[1] * basis[1]) / kept
+    upper_rows = jnp.concatenate([lower_gram, cross], axis=1)
+    normal = nt(upper_rows, upper_rows)
+    beside = nn(upper_rows, jnp.concatenate([cross, upper_gram], axis=0))
+    (inverse,) = inverse_factors([normal], 48, 8, 4)
+    turned = nn(inverse, jnp.concatenate([upper_rows, normal, beside], axis=1))
+    basis, image = turned[:, : 2 * kept], turned[:, 2 * kept :]
+    reduced = nt(image, basis)
+    delta = total(image * basis) / kept
     on_diagonal = lax.broadcasted_iota(jnp.int32, reduced.shape, 0) == lax.broadcasted_iota(jnp.int32, reduced.shape, 1)
-    root, damped = inverse_factors([reduced, reduced + jnp.where(on_diagonal, delta, 0.0)], 8, 4)
+    root, damped = inverse_factors([reduced, reduced + jnp.where(on_diagonal, delta, 0.0)], 32, 8, 4)
     shrunk = nt(reduced, damped)
-    whitened = nn(root, basis[0]), nn(root, basis[1])
-    whitened = jnp.concatenate(whitened, axis=1)
+    whitened = nn(root, basis)
     mixing = nn_parts(shrunk, whitened)
     own_rows = jnp.concatenate([jnp.where(is_upper, cross.T, lower_gram), jnp.where(is_upper, upper_gram, cross)], axis=1)
     scaling = 4.0 * kept / (total(shrunk * shrunk) + 1e-06)
@@ -241,7 +238,7 @@
     first, second = mixing[:, :kept], mixing[:, kept:]
     mixing = stacked(jnp.concatenate([jnp.where(is_upper, second, first), jnp.where(is_upper, first, second)], axis=1))
     coeffs = stacked(coeffs)
-    block = min(width, 512)
+    block = min(width, 1024)
     copies = []
     for k in range(width // block):
         columns = pl.ds(k * block, block)
@@ -266,7 +263,7 @@
         in_specs=[whole] * 4,
         out_specs=(pl.BlockSpec(memory_space=pl.ANY),) * 2,
         out_shape=(jax.ShapeDtypeStruct((kept, width), jnp.float32),) * 2,
-        scratch_shapes=[pltpu.VMEM((kept, width), jnp.float32)] * 2 + [pltpu.SemaphoreType.DMA((2 * max(1, width // 512),))],
+        scratch_shapes=[pltpu.VMEM((kept, width), jnp.float32)] * 2 + [pltpu.SemaphoreType.DMA((2 * max(1, width // 1024),))],
         compiler_params=pltpu.CompilerParams(vmem_limit_bytes=24 << 20),
     )(summed, given, own, other)
 

time: 34.2 us -> 33.4 us (0.977)
  Pallas kernels: 12.2 us -> 11.3 us
    pallas_call x1, Pallas kernels: 11 us -> 10.2 us  [finish(): pl.pallas_call(finish_kernel, in_specs=[whole] * 4, out_specs=(pl.BlockSp...]
where the time goes in v3:
time: 33.4 us; the launch traced here: 33.2 us
  Pallas kernels  11.3 us (34%)
  waiting for transfers between devices  10 us (30%)
  starting transfers between devices  9.87 us (30%)
  local copies, waits for them, and re-layouts  1.22 us (4%)
  between operations  0.66 us (2%)
    pallas_call x1, Pallas kernels, finish(): pl.pallas_call(finish_kernel, in_specs=[whole] * 4, out_specs=(pl.BlockSp...  10.2 us
    ppermute x4, starting transfers between devices, sum_over(): block = block + lax.ppermute(block, (core_axis, axis), route)  8.76 us
    ppermute x4, waiting for transfers between devices, sum_over(): block = block + lax.ppermute(block, (core_axis, axis), route)  8.38 us
    unnamed x2, local copies, waits for them, and re-layouts  1.22 us
    ppermute x1, waiting for transfers between devices, local(): given = lax.ppermute(summed, 'frames', [(0, 1), (1, 0)])  0.91 us
    ppermute x1, waiting for transfers between devices, local(): other = lax.ppermute(frames, 'frames', [(0, 1), (1, 0)])  0.74 us
  transfers between devices with their start and end apart: 6, of which 6 were waited for; matrix products, arithmetic and copies ran while one was open for 0% of the time, Pallas kernels for 2%

profile of v3, /device:TPU:0, one launch (start us, length us, event | category | flops | bytes accessed | tf_op | source)
XLA Modules:
  0.0 33.2 jit_solution(14811037355711024911)
XLA Ops:
  0.6 0.6 %collective-permute-start = (f32[128,2048]{1,0:T(8,128)}, f32[128,2048]{1,0:T(8,128)S(1)}, u32[]{:S(2)}, u32[]{:S(2)}) collective-permute-start(f32[128,2048]{1,0:T(8,128)} %own_ref.1), channel_id=1, source_target_pairs={{0,16},{16,0},{1,17},{17,1},{2,18},{18,2},{3,19},{19,3},{4,20},{20... | collective-permute-start | bytes 3145736 | tf_op jit(solution)/shard_map/ppermute | solution.py:272
  1.2 0.0 copy-start
  1.2 1.2 %copy-done = f32[128,2048]{1,0:T(8,128)S(1)} copy-done((f32[128,2048]{1,0:T(8,128)S(1)}, f32[128,2048]{1,0:T(8,128)}, u32[]{:S(2)}) %copy-start) | copy-done | bytes 1048600
  2.4 0.5 %shard_map.30 = (f32[128,128]{1,0:T(8,128)S(1)}, bf16[256,2048]{1,0:T(8,128)(2,1)S(1)}) custom-call(f32[128,2048]{1,0:T(8,128)S(1)} %copy-done), custom_call_target="tpu_custom_call" | custom-call | flops 402653184 | bytes 2097152 | tf_op jit(solution)/shard_map/pallas_call | solution.py:212
  2.9 0.7 %collective-permute-done.other_ref = f32[128,2048]{1,0:T(8,128)S(1)} collective-permute-done((f32[128,2048]{1,0:T(8,128)}, f32[128,2048]{1,0:T(8,128)S(1)}, u32[]{:S(2)}, u32[]{:S(2)}) %collective-permute-start) | collective-permute-done | bytes 1048608 | tf_op jit(solution)/shard_map/ppermute | solution.py:272
  3.7 0.6 %shard_map.31 = (f32[136,128]{1,0:T(8,128)S(1)}, bf16[256,2048]{1,0:T(8,128)(2,1)S(1)}) custom-call(bf16[256,2048]{1,0:T(8,128)(2,1)S(1)} %get-tuple-element.6.own_ref, f32[128,2048]{1,0:T(8,128)S(1)} %collective-permute-done.other_ref, f32[128,128]{1,0:T(8,128)S(1)} %get-tuple-element.7.own_gram_ref), custom_call_target="tpu_custom_call" | custom-call | flops 402653184 | bytes 2097152 | tf_op jit(solution)/shard_map/pallas_call | solution.py:220
  4.3 3.8 %collective-permute-start.1 = (f32[136,128]{1,0:T(8,128)S(1)}, f32[136,128]{1,0:T(8,128)S(1)}, u32[]{:S(2)}, u32[]{:S(2)}) collective-permute-start(f32[136,128]{1,0:T(8,128)S(1)} %get-tuple-element.8), channel_id=1, source_target_pairs={{0,24},{1,16},{2,19},{3,27},{4,21},{5,29},{6,30},{7,22},{8,25},{9,... | collective-permute-start | bytes 208904 | tf_op jit(solution)/shard_map/ppermute | solution.py:64
  8.1 2.0 %collective-permute-done.1 = f32[136,128]{1,0:T(8,128)S(1)} collective-permute-done((f32[136,128]{1,0:T(8,128)S(1)}, f32[136,128]{1,0:T(8,128)S(1)}, u32[]{:S(2)}, u32[]{:S(2)}) %collective-permute-start.1) | collective-permute-done | bytes 69664 | tf_op jit(solution)/shard_map/ppermute | solution.py:64
  10.1 1.6 %collective-permute-start.2 = (f32[136,128]{1,0:T(8,128)S(1)}, f32[136,128]{1,0:T(8,128)S(1)}, u32[]{:S(2)}, u32[]{:S(2)}) collective-permute-start(f32[136,128]{1,0:T(8,128)S(1)} %add.12), channel_id=1, source_target_pairs={{0,17},{1,25},{2,26},{3,18},{4,28},{5,20},{6,23},{7,31},{8,16},{9,... | collective-permute-start | bytes 208904 | tf_op jit(solution)/shard_map/ppermute | solution.py:64
  11.7 2.2 %collective-permute-done.2 = f32[136,128]{1,0:T(8,128)S(1)} collective-permute-done((f32[136,128]{1,0:T(8,128)S(1)}, f32[136,128]{1,0:T(8,128)S(1)}, u32[]{:S(2)}, u32[]{:S(2)}) %collective-permute-start.2) | collective-permute-done | bytes 69664 | tf_op jit(solution)/shard_map/ppermute | solution.py:64
  13.9 1.6 %collective-permute-start.3 = (f32[136,128]{1,0:T(8,128)S(1)}, f32[136,128]{1,0:T(8,128)S(1)}, u32[]{:S(2)}, u32[]{:S(2)}) collective-permute-start(f32[136,128]{1,0:T(8,128)S(1)} %add.13), channel_id=1, source_target_pairs={{0,18},{1,21},{2,22},{3,17},{4,16},{5,23},{6,20},{7,19},{8,28},{9,... | collective-permute-start | bytes 208904 | tf_op jit(solution)/shard_map/ppermute | solution.py:64
  15.5 2.2 %collective-permute-done.3 = f32[136,128]{1,0:T(8,128)S(1)} collective-permute-done((f32[136,128]{1,0:T(8,128)S(1)}, f32[136,128]{1,0:T(8,128)S(1)}, u32[]{:S(2)}, u32[]{:S(2)}) %collective-permute-start.3) | collective-permute-done | bytes 69664 | tf_op jit(solution)/shard_map/ppermute | solution.py:64
  17.7 1.7 %collective-permute-start.4 = (f32[136,128]{1,0:T(8,128)S(1)}, f32[136,128]{1,0:T(8,128)S(1)}, u32[]{:S(2)}, u32[]{:S(2)}) collective-permute-start(f32[136,128]{1,0:T(8,128)S(1)} %add.14), channel_id=1, source_target_pairs={{0,20},{1,19},{2,16},{3,23},{4,22},{5,17},{6,18},{7,21},{8,26},{9,... | collective-permute-start | bytes 208904 | tf_op jit(solution)/shard_map/ppermute | solution.py:64
  19.5 2.1 %collective-permute-done.4 = f32[136,128]{1,0:T(8,128)S(1)} collective-permute-done((f32[136,128]{1,0:T(8,128)S(1)}, f32[136,128]{1,0:T(8,128)S(1)}, u32[]{:S(2)}, u32[]{:S(2)}) %collective-permute-start.4) | collective-permute-done | bytes 69664 | tf_op jit(solution)/shard_map/ppermute | solution.py:64
  21.5 0.5 %collective-permute-start.5 = (f32[136,128]{1,0:T(8,128)S(1)}, f32[136,128]{1,0:T(8,128)S(1)}, u32[]{:S(2)}, u32[]{:S(2)}) collective-permute-start(f32[136,128]{1,0:T(8,128)S(1)} %add.15.summed_ref), channel_id=1, source_target_pairs={{0,16},{16,0},{1,17},{17,1},{2,18},{18,2},{3,19},{19,3},{4,20},{20... | collective-permute-start | bytes 208904 | tf_op jit(solution)/shard_map/ppermute | solution.py:275
  22.1 0.9 %collective-permute-done.5.given_ref = f32[136,128]{1,0:T(8,128)S(1)} collective-permute-done((f32[136,128]{1,0:T(8,128)S(1)}, f32[136,128]{1,0:T(8,128)S(1)}, u32[]{:S(2)}, u32[]{:S(2)}) %collective-permute-start.5) | collective-permute-done | bytes 69664 | tf_op jit(solution)/shard_map/ppermute | solution.py:275
  23.0 10.2 %shard_map.32 = (f32[128,2048]{1,0:T(8,128)}, f32[128,2048]{1,0:T(8,128)}) custom-call(f32[136,128]{1,0:T(8,128)S(1)} %add.15.summed_ref, f32[136,128]{1,0:T(8,128)S(1)} %collective-permute-done.5.given_ref, bf16[256,2048]{1,0:T(8,128)(2,1)S(1)} %get-tuple-element.6.own_ref, bf16[256,2048]{1,0:T(8,128)(2,1)S(1)} %get-tuple-element.9.other_ref), custom_call_target="tpu_custom_call" | custom-call | tf_op jit(solution)/shard_map/pallas_call | solution.py:261
  (4 shorter events, 0.0 us)
Async XLA Ops:
  0.6 3.1 %collective-permute-start = (f32[128,2048]{1,0:T(8,128)}, f32[128,2048]{1,0:T(8,128)S(1)}, u32[]{:S(2)}, u32[]{:S(2)}) collective-permute-start(f32[128,2048]{1,0:T(8,128)} %own_ref.1), channel_id=1, source_target_pairs={{0,16},{16,0},{1,17},{17,1},{2,18},{18,2},{3,19},{19,3},{4,20},{20... | collective-permute-start | bytes 3145736 | tf_op jit(solution)/shard_map/ppermute | solution.py:272
  1.2 1.2 %copy-start = (f32[128,2048]{1,0:T(8,128)S(1)}, f32[128,2048]{1,0:T(8,128)}, u32[]{:S(2)}) copy-start(f32[128,2048]{1,0:T(8,128)} %own_ref.1) | copy-start | bytes 3145732
  4.3 5.7 %collective-permute-start.1 = (f32[136,128]{1,0:T(8,128)S(1)}, f32[136,128]{1,0:T(8,128)S(1)}, u32[]{:S(2)}, u32[]{:S(2)}) collective-permute-start(f32[136,128]{1,0:T(8,128)S(1)} %get-tuple-element.8), channel_id=1, source_target_pairs={{0,24},{1,16},{2,19},{3,27},{4,21},{5,29},{6,30},{7,22},{8,25},{9,... | collective-permute-start | bytes 208904 | tf_op jit(solution)/shard_map/ppermute | solution.py:64
  10.1 3.8 %collective-permute-start.2 = (f32[136,128]{1,0:T(8,128)S(1)}, f32[136,128]{1,0:T(8,128)S(1)}, u32[]{:S(2)}, u32[]{:S(2)}) collective-permute-start(f32[136,128]{1,0:T(8,128)S(1)} %add.12), channel_id=1, source_target_pairs={{0,17},{1,25},{2,26},{3,18},{4,28},{5,20},{6,23},{7,31},{8,16},{9,... | collective-permute-start | bytes 208904 | tf_op jit(solution)/shard_map/ppermute | solution.py:64
  13.9 3.8 %collective-permute-start.3 = (f32[136,128]{1,0:T(8,128)S(1)}, f32[136,128]{1,0:T(8,128)S(1)}, u32[]{:S(2)}, u32[]{:S(2)}) collective-permute-start(f32[136,128]{1,0:T(8,128)S(1)} %add.13), channel_id=1, source_target_pairs={{0,18},{1,21},{2,22},{3,17},{4,16},{5,23},{6,20},{7,19},{8,28},{9,... | collective-permute-start | bytes 208904 | tf_op jit(solution)/shard_map/ppermute | solution.py:64
  17.7 3.8 %collective-permute-start.4 = (f32[136,128]{1,0:T(8,128)S(1)}, f32[136,128]{1,0:T(8,128)S(1)}, u32[]{:S(2)}, u32[]{:S(2)}) collective-permute-start(f32[136,128]{1,0:T(8,128)S(1)} %add.14), channel_id=1, source_target_pairs={{0,20},{1,19},{2,16},{3,23},{4,22},{5,17},{6,18},{7,21},{8,26},{9,... | collective-permute-start | bytes 208904 | tf_op jit(solution)/shard_map/ppermute | solution.py:64
  21.5 1.5 %collective-permute-start.5 = (f32[136,128]{1,0:T(8,128)S(1)}, f32[136,128]{1,0:T(8,128)S(1)}, u32[]{:S(2)}, u32[]{:S(2)}) collective-permute-start(f32[136,128]{1,0:T(8,128)S(1)} %add.15.summed_ref), channel_id=1, source_target_pairs={{0,16},{16,0},{1,17},{17,1},{2,18},{18,2},{3,19},{19,3},{4,20},{20... | collective-permute-start | bytes 208904 | tf_op jit(solution)/shard_map/ppermute | solution.py:275

commit v4 on v3

--- a/solution.py
+++ b/solution.py
@@ -4,6 +4,9 @@
 from jax.experimental import pallas as pl
 from jax.experimental.pallas import tpu as pltpu
 from jax.sharding import PartitionSpec as P
+
+PIECES = 2
+
 
 def nn(left, right):
     return lax.dot_general(left, right, (((1,), (0,)), ((), ())), precision=lax.Precision.HIGHEST, preferred_element_type=jnp.float32)
@@ -120,11 +123,16 @@
             z[first:rest], above = eliminate(block, 8 * first, [z[first:rest], block], group, ahead)
             above = jnp.concatenate(above, axis=0)
             both = jnp.concatenate([above, jnp.concatenate(z[first:rest], axis=0)], axis=1)
-            update = nn(above.T[8 * rest :], both)
-            for i in range(rest, count):
-                rows = slice(8 * (i - rest), 8 * (i - rest) + 8)
-                a[i] = a[i] - update[rows, :size]
-                z[i] = z[i] - update[rows, size:]
+            turned = above.T
+            soon = min(rest + step, count)
+            for low, high in ((rest, soon), (soon, count)):
+                if low == high:
+                    continue
+                update = nn(turned[8 * low : 8 * high], both)
+                for i in range(low, high):
+                    rows = slice(8 * (i - low), 8 * (i - low) + 8)
+                    a[i] = a[i] - update[rows, :size]
+                    z[i] = z[i] - update[rows, size:]
     return [jnp.concatenate(z, axis=0) for z in right]
 
 
@@ -144,8 +152,8 @@
     delta = total(image * basis) / kept
     on_diagonal = lax.broadcasted_iota(jnp.int32, reduced.shape, 0) == lax.broadcasted_iota(jnp.int32, reduced.shape, 1)
     root, damped = inverse_factors([reduced, reduced + jnp.where(on_diagonal, delta, 0.0)], 32, 8, 4)
-    shrunk = nt(reduced, damped)
-    whitened = nn(root, basis)
+    shrunk = nt_parts(reduced, damped)
+    whitened = nn_parts(root, basis)
     mixing = nn_parts(shrunk, whitened)
     own_rows = jnp.concatenate([jnp.where(is_upper, cross.T, lower_gram), jnp.where(is_upper, upper_gram, cross)], axis=1)
     scaling = 4.0 * kept / (total(shrunk * shrunk) + 1e-06)
@@ -238,18 +246,17 @@
     first, second = mixing[:, :kept], mixing[:, kept:]
     mixing = stacked(jnp.concatenate([jnp.where(is_upper, second, first), jnp.where(is_upper, first, second)], axis=1))
     coeffs = stacked(coeffs)
-    block = min(width, 1024)
-    copies = []
-    for k in range(width // block):
-        columns = pl.ds(k * block, block)
-        high = jnp.concatenate([own_ref[:kept, columns], other_ref[:kept, columns]], axis=0)
-        low = jnp.concatenate([own_ref[kept:, columns], other_ref[kept:, columns]], axis=0)
-        sketch = product(mixing, high, low)
-        sketch_buf[:, columns] = sketch
-        copies.append(pltpu.make_async_copy(sketch_buf.at[:, columns], sketch_ref.at[:, columns], sems.at[2 * k]))
-        copies[-1].start()
-        projected_buf[:, columns] = product(coeffs, *split(sketch))
-        copies.append(pltpu.make_async_copy(projected_buf.at[:, columns], projected_ref.at[:, columns], sems.at[2 * k + 1]))
+    high = jnp.concatenate([own_ref[:kept], other_ref[:kept]], axis=0)
+    low = jnp.concatenate([own_ref[kept:], other_ref[kept:]], axis=0)
+    sketch = product(mixing, high, low)
+    sketch_buf[...] = sketch
+    copies = [pltpu.make_async_copy(sketch_buf, sketch_ref, sems.at[0])]
+    copies[0].start()
+    block = width // PIECES
+    for k in range(PIECES):
+        columns = slice(k * block, (k + 1) * block)
+        projected_buf[:, columns] = product(coeffs, *split(sketch[:, columns]))
+        copies.append(pltpu.make_async_copy(projected_buf.at[:, columns], projected_ref.at[:, columns], sems.at[k + 1]))
         copies[-1].start()
     for copy in copies:
         copy.wait()
@@ -263,7 +270,7 @@
         in_specs=[whole] * 4,
         out_specs=(pl.BlockSpec(memory_space=pl.ANY),) * 2,
         out_shape=(jax.ShapeDtypeStruct((kept, width), jnp.float32),) * 2,
-        scratch_shapes=[pltpu.VMEM((kept, width), jnp.float32)] * 2 + [pltpu.SemaphoreType.DMA((2 * max(1, width // 1024),))],
+        scratch_shapes=[pltpu.VMEM((kept, width), jnp.float32)] * 2 + [pltpu.SemaphoreType.DMA((PIECES + 1,))],
         compiler_params=pltpu.CompilerParams(vmem_limit_bytes=24 << 20),
     )(summed, given, own, other)
 

time: 33.4 us -> 33.2 us (level)
  no operation moved by 1% of the time
where the time goes in v4:
time: 33.2 us; the launch traced here: 33 us
  Pallas kernels  11.2 us (34%)
  waiting for transfers between devices  10 us (30%)
  starting transfers between devices  9.87 us (30%)
  local copies, waits for them, and re-layouts  1.22 us (4%)
  between operations  0.66 us (2%)
    pallas_call x1, Pallas kernels, finish(): pl.pallas_call(finish_kernel, in_specs=[whole] * 4, out_specs=(pl.BlockSp...  10 us
    ppermute x4, starting transfers between devices, sum_over(): block = block + lax.ppermute(block, (core_axis, axis), route)  8.76 us
    ppermute x4, waiting for transfers between devices, sum_over(): block = block + lax.ppermute(block, (core_axis, axis), route)  8.38 us
    unnamed x2, local copies, waits for them, and re-layouts  1.22 us
    ppermute x1, waiting for transfers between devices, local(): given = lax.ppermute(summed, 'frames', [(0, 1), (1, 0)])  0.91 us
    ppermute x1, waiting for transfers between devices, local(): other = lax.ppermute(frames, 'frames', [(0, 1), (1, 0)])  0.74 us
  transfers between devices with their start and end apart: 6, of which 6 were waited for; matrix products, arithmetic and copies ran while one was open for 0% of the time, Pallas kernels for 2%

profile of v4, /device:TPU:0, one launch (start us, length us, event | category | flops | bytes accessed | tf_op | source)
XLA Modules:
  0.0 33.0 jit_solution(12124913694318939385)
XLA Ops:
  0.6 0.6 %collective-permute-start = (f32[128,2048]{1,0:T(8,128)}, f32[128,2048]{1,0:T(8,128)S(1)}, u32[]{:S(2)}, u32[]{:S(2)}) collective-permute-start(f32[128,2048]{1,0:T(8,128)} %own_ref.1), channel_id=1, source_target_pairs={{0,16},{16,0},{1,17},{17,1},{2,18},{18,2},{3,19},{19,3},{4,20},{20... | collective-permute-start | bytes 3145736 | tf_op jit(solution)/shard_map/ppermute | solution.py:279
  1.2 0.0 copy-start
  1.2 1.2 %copy-done = f32[128,2048]{1,0:T(8,128)S(1)} copy-done((f32[128,2048]{1,0:T(8,128)S(1)}, f32[128,2048]{1,0:T(8,128)}, u32[]{:S(2)}) %copy-start) | copy-done | bytes 1048600
  2.4 0.5 %shard_map.30 = (f32[128,128]{1,0:T(8,128)S(1)}, bf16[256,2048]{1,0:T(8,128)(2,1)S(1)}) custom-call(f32[128,2048]{1,0:T(8,128)S(1)} %copy-done), custom_call_target="tpu_custom_call" | custom-call | flops 402653184 | bytes 2097152 | tf_op jit(solution)/shard_map/pallas_call | solution.py:220
  2.9 0.7 %collective-permute-done.other_ref = f32[128,2048]{1,0:T(8,128)S(1)} collective-permute-done((f32[128,2048]{1,0:T(8,128)}, f32[128,2048]{1,0:T(8,128)S(1)}, u32[]{:S(2)}, u32[]{:S(2)}) %collective-permute-start) | collective-permute-done | bytes 1048608 | tf_op jit(solution)/shard_map/ppermute | solution.py:279
  3.7 0.6 %shard_map.31 = (f32[136,128]{1,0:T(8,128)S(1)}, bf16[256,2048]{1,0:T(8,128)(2,1)S(1)}) custom-call(bf16[256,2048]{1,0:T(8,128)(2,1)S(1)} %get-tuple-element.6.own_ref, f32[128,2048]{1,0:T(8,128)S(1)} %collective-permute-done.other_ref, f32[128,128]{1,0:T(8,128)S(1)} %get-tuple-element.7.own_gram_ref), custom_call_target="tpu_custom_call" | custom-call | flops 402653184 | bytes 2097152 | tf_op jit(solution)/shard_map/pallas_call | solution.py:228
  4.3 3.8 %collective-permute-start.1 = (f32[136,128]{1,0:T(8,128)S(1)}, f32[136,128]{1,0:T(8,128)S(1)}, u32[]{:S(2)}, u32[]{:S(2)}) collective-permute-start(f32[136,128]{1,0:T(8,128)S(1)} %get-tuple-element.8), channel_id=1, source_target_pairs={{0,24},{1,16},{2,19},{3,27},{4,21},{5,29},{6,30},{7,22},{8,25},{9,... | collective-permute-start | bytes 208904 | tf_op jit(solution)/shard_map/ppermute | solution.py:67
  8.1 2.0 %collective-permute-done.1 = f32[136,128]{1,0:T(8,128)S(1)} collective-permute-done((f32[136,128]{1,0:T(8,128)S(1)}, f32[136,128]{1,0:T(8,128)S(1)}, u32[]{:S(2)}, u32[]{:S(2)}) %collective-permute-start.1) | collective-permute-done | bytes 69664 | tf_op jit(solution)/shard_map/ppermute | solution.py:67
  10.1 1.6 %collective-permute-start.2 = (f32[136,128]{1,0:T(8,128)S(1)}, f32[136,128]{1,0:T(8,128)S(1)}, u32[]{:S(2)}, u32[]{:S(2)}) collective-permute-start(f32[136,128]{1,0:T(8,128)S(1)} %add.12), channel_id=1, source_target_pairs={{0,17},{1,25},{2,26},{3,18},{4,28},{5,20},{6,23},{7,31},{8,16},{9,... | collective-permute-start | bytes 208904 | tf_op jit(solution)/shard_map/ppermute | solution.py:67
  11.7 2.2 %collective-permute-done.2 = f32[136,128]{1,0:T(8,128)S(1)} collective-permute-done((f32[136,128]{1,0:T(8,128)S(1)}, f32[136,128]{1,0:T(8,128)S(1)}, u32[]{:S(2)}, u32[]{:S(2)}) %collective-permute-start.2) | collective-permute-done | bytes 69664 | tf_op jit(solution)/shard_map/ppermute | solution.py:67
  13.9 1.6 %collective-permute-start.3 = (f32[136,128]{1,0:T(8,128)S(1)}, f32[136,128]{1,0:T(8,128)S(1)}, u32[]{:S(2)}, u32[]{:S(2)}) collective-permute-start(f32[136,128]{1,0:T(8,128)S(1)} %add.13), channel_id=1, source_target_pairs={{0,18},{1,21},{2,22},{3,17},{4,16},{5,23},{6,20},{7,19},{8,28},{9,... | collective-permute-start | bytes 208904 | tf_op jit(solution)/shard_map/ppermute | solution.py:67
  15.5 2.2 %collective-permute-done.3 = f32[136,128]{1,0:T(8,128)S(1)} collective-permute-done((f32[136,128]{1,0:T(8,128)S(1)}, f32[136,128]{1,0:T(8,128)S(1)}, u32[]{:S(2)}, u32[]{:S(2)}) %collective-permute-start.3) | collective-permute-done | bytes 69664 | tf_op jit(solution)/shard_map/ppermute | solution.py:67
  17.7 1.7 %collective-permute-start.4 = (f32[136,128]{1,0:T(8,128)S(1)}, f32[136,128]{1,0:T(8,128)S(1)}, u32[]{:S(2)}, u32[]{:S(2)}) collective-permute-start(f32[136,128]{1,0:T(8,128)S(1)} %add.14), channel_id=1, source_target_pairs={{0,20},{1,19},{2,16},{3,23},{4,22},{5,17},{6,18},{7,21},{8,26},{9,... | collective-permute-start | bytes 208904 | tf_op jit(solution)/shard_map/ppermute | solution.py:67
  19.5 2.1 %collective-permute-done.4 = f32[136,128]{1,0:T(8,128)S(1)} collective-permute-done((f32[136,128]{1,0:T(8,128)S(1)}, f32[136,128]{1,0:T(8,128)S(1)}, u32[]{:S(2)}, u32[]{:S(2)}) %collective-permute-start.4) | collective-permute-done | bytes 69664 | tf_op jit(solution)/shard_map/ppermute | solution.py:67
  21.5 0.5 %collective-permute-start.5 = (f32[136,128]{1,0:T(8,128)S(1)}, f32[136,128]{1,0:T(8,128)S(1)}, u32[]{:S(2)}, u32[]{:S(2)}) collective-permute-start(f32[136,128]{1,0:T(8,128)S(1)} %add.15.summed_ref), channel_id=1, source_target_pairs={{0,16},{16,0},{1,17},{17,1},{2,18},{18,2},{3,19},{19,3},{4,20},{20... | collective-permute-start | bytes 208904 | tf_op jit(solution)/shard_map/ppermute | solution.py:282
  22.1 0.9 %collective-permute-done.5.given_ref = f32[136,128]{1,0:T(8,128)S(1)} collective-permute-done((f32[136,128]{1,0:T(8,128)S(1)}, f32[136,128]{1,0:T(8,128)S(1)}, u32[]{:S(2)}, u32[]{:S(2)}) %collective-permute-start.5) | collective-permute-done | bytes 69664 | tf_op jit(solution)/shard_map/ppermute | solution.py:282
  23.0 10.0 %shard_map.32 = (f32[128,2048]{1,0:T(8,128)}, f32[128,2048]{1,0:T(8,128)}) custom-call(f32[136,128]{1,0:T(8,128)S(1)} %add.15.summed_ref, f32[136,128]{1,0:T(8,128)S(1)} %collective-permute-done.5.given_ref, bf16[256,2048]{1,0:T(8,128)(2,1)S(1)} %get-tuple-element.6.own_ref, bf16[256,2048]{1,0:T(8,128)(2,1)S(1)} %get-tuple-element.9.other_ref), custom_call_target="tpu_custom_call" | custom-call | tf_op jit(solution)/shard_map/pallas_call | solution.py:268
  (4 shorter events, 0.0 us)
Async XLA Ops:
  0.6 3.1 %collective-permute-start = (f32[128,2048]{1,0:T(8,128)}, f32[128,2048]{1,0:T(8,128)S(1)}, u32[]{:S(2)}, u32[]{:S(2)}) collective-permute-start(f32[128,2048]{1,0:T(8,128)} %own_ref.1), channel_id=1, source_target_pairs={{0,16},{16,0},{1,17},{17,1},{2,18},{18,2},{3,19},{19,3},{4,20},{20... | collective-permute-start | bytes 3145736 | tf_op jit(solution)/shard_map/ppermute | solution.py:279
  1.2 1.2 %copy-start = (f32[128,2048]{1,0:T(8,128)S(1)}, f32[128,2048]{1,0:T(8,128)}, u32[]{:S(2)}) copy-start(f32[128,2048]{1,0:T(8,128)} %own_ref.1) | copy-start | bytes 3145732
  4.3 5.7 %collective-permute-start.1 = (f32[136,128]{1,0:T(8,128)S(1)}, f32[136,128]{1,0:T(8,128)S(1)}, u32[]{:S(2)}, u32[]{:S(2)}) collective-permute-start(f32[136,128]{1,0:T(8,128)S(1)} %get-tuple-element.8), channel_id=1, source_target_pairs={{0,24},{1,16},{2,19},{3,27},{4,21},{5,29},{6,30},{7,22},{8,25},{9,... | collective-permute-start | bytes 208904 | tf_op jit(solution)/shard_map/ppermute | solution.py:67
  10.1 3.8 %collective-permute-start.2 = (f32[136,128]{1,0:T(8,128)S(1)}, f32[136,128]{1,0:T(8,128)S(1)}, u32[]{:S(2)}, u32[]{:S(2)}) collective-permute-start(f32[136,128]{1,0:T(8,128)S(1)} %add.12), channel_id=1, source_target_pairs={{0,17},{1,25},{2,26},{3,18},{4,28},{5,20},{6,23},{7,31},{8,16},{9,... | collective-permute-start | bytes 208904 | tf_op jit(solution)/shard_map/ppermute | solution.py:67
  13.9 3.8 %collective-permute-start.3 = (f32[136,128]{1,0:T(8,128)S(1)}, f32[136,128]{1,0:T(8,128)S(1)}, u32[]{:S(2)}, u32[]{:S(2)}) collective-permute-start(f32[136,128]{1,0:T(8,128)S(1)} %add.13), channel_id=1, source_target_pairs={{0,18},{1,21},{2,22},{3,17},{4,16},{5,23},{6,20},{7,19},{8,28},{9,... | collective-permute-start | bytes 208904 | tf_op jit(solution)/shard_map/ppermute | solution.py:67
  17.7 3.8 %collective-permute-start.4 = (f32[136,128]{1,0:T(8,128)S(1)}, f32[136,128]{1,0:T(8,128)S(1)}, u32[]{:S(2)}, u32[]{:S(2)}) collective-permute-start(f32[136,128]{1,0:T(8,128)S(1)} %add.14), channel_id=1, source_target_pairs={{0,20},{1,19},{2,16},{3,23},{4,22},{5,17},{6,18},{7,21},{8,26},{9,... | collective-permute-start | bytes 208904 | tf_op jit(solution)/shard_map/ppermute | solution.py:67
  21.5 1.5 %collective-permute-start.5 = (f32[136,128]{1,0:T(8,128)S(1)}, f32[136,128]{1,0:T(8,128)S(1)}, u32[]{:S(2)}, u32[]{:S(2)}) collective-permute-start(f32[136,128]{1,0:T(8,128)S(1)} %add.15.summed_ref), channel_id=1, source_target_pairs={{0,16},{16,0},{1,17},{17,1},{2,18},{18,2},{3,19},{19,3},{4,20},{20... | collective-permute-start | bytes 208904 | tf_op jit(solution)/shard_map/ppermute | solution.py:282
